TPU v7x, 128 devices: a whole 4x4x4 slice. The times are simulated.
128 devices in a mesh: rep: 1, r: 4 (over x), s: 32 (over y, z, core).
Axes of the slice: x: 4, y: 4, z: 4, core: 2. Of those that a mesh axis runs over, the one named last changes fastest.
Arguments:
- x: bfloat16 [128, 2048, 1280], P(('rep', 'r', 's'))
- dy: bfloat16 [128, 2048, 1280], P(('rep', 'r', 's'))
- w_gate: bfloat16 [2, 1280, 4864], P(None, 's')
- w_up: bfloat16 [2, 1280, 4864], P(None, 's')
- w_down: bfloat16 [2, 4864, 1280], P(None, 's')
- m_w_gate: float32 [2, 1280, 4864], P(None, 's')
- m_w_up: float32 [2, 1280, 4864], P(None, 's')
- m_w_down: float32 [2, 4864, 1280], P(None, 's')
- v_w_gate: float32 [2, 1280, 4864], P(None, 's')
- v_w_up: float32 [2, 1280, 4864], P(None, 's')
- v_w_down: float32 [2, 4864, 1280], P(None, 's')
Outputs:
- output 1: bfloat16 [2, 1280, 4864], P('rep', 's')
- output 2: bfloat16 [2, 1280, 4864], P('rep', 's')
- output 3: bfloat16 [2, 4864, 1280], P('rep', 's')
- output 4: float32 [2, 1280, 4864], P('rep', 's')
- output 5: float32 [2, 1280, 4864], P('rep', 's')
- output 6: float32 [2, 4864, 1280], P('rep', 's')
- output 7: float32 [2, 1280, 4864], P('rep', 's')
- output 8: float32 [2, 1280, 4864], P('rep', 's')
- output 9: float32 [2, 4864, 1280], P('rep', 's')
All inputs are finite; a program needn't handle non-finite values.
Results may differ from a plain program's by a relative error of at most 0.022.
Values are sent between devices in bfloat16 or wider.
A program may use at most 1.5 GiB of HBM per device.

v0:
```python
import jax
import jax.numpy as jnp
from jax import lax
from jax.sharding import PartitionSpec as P

NAMES = ("w_gate", "w_up", "w_down")


def matmul(a, w):
    return jnp.dot(a, w, preferred_element_type=jnp.float32).astype(jnp.bfloat16)


def normed(h):
    wide = h.astype(jnp.float32)
    scale = lax.rsqrt(jnp.mean(wide**2, -1, keepdims=True) + 1e-6)
    return (wide * scale).astype(jnp.bfloat16)


def layer(h, w):
    a = normed(h)
    gate = jnp.dot(a, w["w_gate"], preferred_element_type=jnp.float32)
    up = jnp.dot(a, w["w_up"], preferred_element_type=jnp.float32)
    return h + matmul((jax.nn.silu(gate) * up).astype(jnp.bfloat16), w["w_down"])


def adamw(w, m, v, g):
    m = 0.9 * m + 0.1 * g
    v = 0.95 * v + 0.05 * g * g
    step = m * lax.rsqrt(v + 1e-8) + 0.1 * w
    return (w - 0.02 * step).astype(jnp.bfloat16), m, v


def clipped(gradients, sum_of_squares, count):
    factor = jnp.minimum(1.0, 0.5 * lax.rsqrt(sum_of_squares / count + 1e-30))
    return [g * factor for g in gradients]


def solution(mesh):
    def fetched(weights, number):
        return {name: lax.all_gather(w[number], "s", axis=0, tiled=True) for name, w in zip(NAMES, weights, strict=True)}

    def summed(term):
        return lax.psum(lax.psum_scatter(term, "s", scatter_dimension=0, tiled=True), "r")

    def step(x, dy, *arrays):
        weights, m, v = (arrays[i : i + 3] for i in (0, 3, 6))
        layers = weights[0].shape[0]
        h, kept = x[0], []
        for number in range(layers):
            kept.append(h)
            h = layer(h, fetched(weights, number))
        by_h, mine = dy[0], [None] * layers
        for number in reversed(range(layers)):
            _, back = jax.vjp(lambda w, h: layer(h, w), fetched(weights, number), kept[number])
            by_w, by_h = back(by_h)
            mine[number] = [summed(by_w[name]) for name in NAMES]
        gradients = [jnp.stack([mine[number][i] for number in range(layers)]).astype(jnp.float32) for i in range(3)]
        squares = lax.psum(sum(jnp.sum(g * g) for g in gradients), "s")
        gradients = clipped(gradients, squares, lax.psum(1, "s") * sum(g.size for g in gradients))
        new = [adamw(w.astype(jnp.float32), m, v, g) for w, m, v, g in zip(weights, m, v, gradients, strict=True)]
        return tuple(one[which] for which in range(3) for one in new)

    states, cut = P(("rep", "r", "s"), None, None), P(None, "s", None)
    return jax.shard_map(
        step,
        mesh=mesh,
        in_specs=(states, states) + (cut,) * 9,
        out_specs=(P("rep", "s", None),) * 9,
        check_vma=False,
    )
```

profile of v0, /device:TPU:1, one launch (start us, length us, event | category | flops | bytes accessed | tf_op | source)
XLA Modules:
  0.0 1356.7 jit_solution(2828041397135304479)
XLA Ops:
  34.8 41.9 %all-gather.13.cloned.1.call-done = bf16[1,1280,4864]{2,1,0:T(8,128)(2,1)} async-done(((bf16[1,40,4864]{2,1,0:T(8,128)(2,1)}), bf16[1,1280,4864]{2,1,0:T(8,128)(2,1)}) %all-gather.13.cloned.1.call-update) | async-done | bytes 12451856 | tf_op jit(solution)/shard_map/all_gather | solution.py:40
  76.8 34.4 %fusion.34 = f32[2048,4864]{1,0:T(8,128)} fusion(bf16[1,1280,4864]{2,1,0:T(8,128)(2,1)} %all-gather.13.cloned.1.call-done, bf16[1,2048,1280]{1,2,0:T(8,128)(2,1)} %copy.20, f32[2048]{0:T(1024)S(1)} %add_rsqrt_fusion), kind=kOutput, calls=%fused_computation.52 | convolution fusion | flops 25509232640 | bytes 57548800 | tf_op jit(solution)/shard_map/dot_general | solution.py:21
  111.1 30.2 %all-gather.15.cloned.1.call-done = bf16[1,1280,4864]{2,1,0:T(8,128)(2,1)} async-done(((bf16[1,40,4864]{2,1,0:T(8,128)(2,1)}), bf16[1,1280,4864]{2,1,0:T(8,128)(2,1)}) %all-gather.15.cloned.1.call-update) | async-done | bytes 12451856 | tf_op jit(solution)/shard_map/all_gather | solution.py:40
  141.3 48.5 %multiply_convert_fusion.1 = (bf16[2048,4864]{1,0:T(8,128)(2,1)}, f32[2048,4864]{1,0:T(8,128)}) fusion(f32[2048,4864]{1,0:T(8,128)} %fusion.34, bf16[1,1280,4864]{2,1,0:T(8,128)(2,1)} %all-gather.15.cloned.1.call-done, bf16[1,2048,1280]{1,2,0:T(8,128)(2,1)} %copy.20, f32[2048]{0:T(1024)S(1)} %add_rsqrt_fusion), kind=kOutput, calls=%fused_computation.17 | convolution fusion | flops 25569001472 | bytes 117317632 | tf_op jit(solution)/shard_map/dot_general | solution.py:22
  205.9 46.1 %fusion.40 = (f32[2048]{0:T(1024)S(1)}, bf16[2048,1280]{0,1:T(8,128)(2,1)}) fusion(bf16[2048,4864]{1,0:T(8,128)(2,1)} %get-tuple-element.30, bf16[1,4864,1280]{2,1,0:T(8,128)(2,1)} %all-gather.17.cloned.1.call-done, bf16[1,2048,1280]{1,2,0:T(8,128)(2,1)} %copy.20), kind=kOutput, calls=%fused_computation.58 | convolution fusion | flops 25514473472 | bytes 42868736 | tf_op jit(solution)/shard_map/dot_general | solution.py:10
  270.4 34.3 %convolution_convert_fusion.1 = bf16[2048,4864]{1,0:T(8,128)(2,1)} fusion(bf16[1,4864,1280]{2,1,0:T(8,128)(2,1)} %all-gather.21.cloned.1.call-done, bf16[1,2048,1280]{2,1,0:T(8,128)(2,1)} %param.12), kind=kOutput, calls=%fused_computation.29 | convolution fusion | flops 25511329792 | bytes 37617664 | tf_op jit(solution)/shard_map/transpose(jvp())/dot_general | solution.py:10
  304.7 30.2 %all-gather.23.cloned.1.call-done = bf16[1,1280,4864]{2,1,0:T(8,128)(2,1)} async-done(((bf16[1,40,4864]{2,1,0:T(8,128)(2,1)}), bf16[1,1280,4864]{2,1,0:T(8,128)(2,1)}) %all-gather.23.cloned.1.call-update) | async-done | bytes 12451856 | tf_op jit(solution)/shard_map/all_gather | solution.py:40
  334.9 34.4 %fusion.21 = f32[2048,4864]{1,0:T(8,128)} fusion(bf16[1,1280,4864]{2,1,0:T(8,128)(2,1)} %all-gather.23.cloned.1.call-done, bf16[2048,1280]{0,1:T(8,128)(2,1)} %get-tuple-element.33, f32[2048]{0:T(1024)S(1)} %fusion.91), kind=kOutput, calls=%fused_computation.39 | convolution fusion | flops 25509232640 | bytes 57548800 | tf_op jit(solution)/shard_map/jvp()/dot_general | solution.py:22
  399.3 55.5 %fusion.2 = (bf16[2048,4864]{1,0:T(8,128)(2,1)}, f32[2048,4864]{1,0:T(8,128)}) fusion(f32[2048,4864]{1,0:T(8,128)} %fusion.21, bf16[2048,4864]{1,0:T(8,128)(2,1)} %convolution_convert_fusion.1, bf16[1,1280,4864]{2,1,0:T(8,128)(2,1)} %all-gather.19.cloned.1.call-done, bf16[2048,1280]{0,1:T(8,128)(2,1)} %get-tuple-element.33, f32[2048]{0:T(1024)S(1)} %fusion.91), kind=kOutput, calls=%fused_computation.8 | convolution fusion | flops 25628770304 | bytes 137240576 | tf_op jit(solution)/shard_map/jvp()/dot_general | solution.py:21
  454.8 37.0 %fusion.46 = bf16[2048,1280]{0,1:T(8,128)(2,1)} fusion(bf16[1,1280,4864]{2,1,0:T(8,128)(2,1)} %all-gather.23.cloned.1.call-done, bf16[2048,4864]{1,0:T(8,128)(2,1)} %convolution_convert_fusion.1, f32[2048,4864]{1,0:T(8,128)} %get-tuple-element.35), kind=kOutput, calls=%fused_computation.62 | convolution fusion | flops 25563758592 | bytes 77463552 | tf_op jit(solution)/shard_map/transpose(jvp())/dot_general | solution.py:22
  491.9 36.0 %fusion.42 = (f32[2048]{0:T(1024)S(1)}, bf16[2048,1280]{0,1:T(8,128)(2,1)}) fusion(bf16[2048,1280]{0,1:T(8,128)(2,1)} %get-tuple-element.33, bf16[2048,1280]{0,1:T(8,128)(2,1)} %fusion.46, bf16[2048,4864]{1,0:T(8,128)(2,1)} %get-tuple-element.34, bf16[1,1280,4864]{2,1,0:T(8,128)(2,1)} %all-gather.19.cloned.1.call-done), kind=kOutput, calls=%fused_computation.60 | convolution fusion | flops 25514473472 | bytes 48111616 | tf_op jit(solution)/shard_map/transpose(jvp())/dot_general | solution.py:21
  540.2 33.8 %convolution_convert_fusion.2 = bf16[4864,1280]{1,0:T(8,128)(2,1)} fusion(bf16[2048,4864]{1,0:T(8,128)(2,1)} %get-tuple-element.30, bf16[2048,1280]{0,1:T(8,128)(2,1)} %fusion.59), kind=kOutput, calls=%fused_computation.30 | convolution fusion | flops 25507594240 | bytes 37617664 | tf_op jit(solution)/shard_map/transpose(jvp())/dot_general | solution.py:10
  574.1 41.6 %fusion.18 = bf16[4864,1280]{1,0:T(8,128)(2,1)} fusion(f32[2048,4864]{1,0:T(8,128)} %fusion.21, bf16[1,2048,1280]{2,1,0:T(8,128)(2,1)} %param.12, f32[2048,4864]{1,0:T(8,128)} %get-tuple-element.35), kind=kOutput, calls=%fused_computation.25 | convolution fusion | flops 25567363072 | bytes 97386496 | tf_op jit(solution)/shard_map/transpose(jvp())/dot_general | solution.py:10
  615.8 34.0 %convolution_convert_fusion = bf16[2048,4864]{1,0:T(8,128)(2,1)} fusion(bf16[2048,1280]{0,1:T(8,128)(2,1)} %fusion.59, bf16[1,4864,1280]{2,1,0:T(8,128)(2,1)} %all-gather.17.cloned.1.call-done), kind=kOutput, calls=%fused_computation.28 | convolution fusion | flops 25511329792 | bytes 37617664 | tf_op jit(solution)/shard_map/transpose(jvp())/dot_general | solution.py:10
  649.9 37.8 %fusion.20 = bf16[1280,4864]{1,0:T(8,128)(2,1)} fusion(bf16[2048,4864]{1,0:T(8,128)(2,1)} %convolution_convert_fusion, f32[2048,4864]{1,0:T(8,128)} %fusion.34, bf16[1,2048,1280]{1,2,0:T(8,128)(2,1)} %copy.20, f32[2048]{0:T(1024)S(1)} %copy-done.12), kind=kOutput, calls=%fused_computation.27 | convolution fusion | flops 25575227392 | bytes 77471744 | tf_op jit(solution)/shard_map/transpose(jvp())/dot_general | solution.py:22
  688.4 37.8 %fusion.19 = bf16[1280,4864]{1,0:T(8,128)(2,1)} fusion(bf16[2048,4864]{1,0:T(8,128)(2,1)} %convolution_convert_fusion.1, bf16[2048,1280]{0,1:T(8,128)(2,1)} %get-tuple-element.33, f32[2048]{0:T(1024)S(1)} %copy-done.8, f32[2048,4864]{1,0:T(8,128)} %get-tuple-element.35), kind=kOutput, calls=%fused_computation.26 | convolution fusion | flops 25575227392 | bytes 77471744 | tf_op jit(solution)/shard_map/transpose(jvp())/dot_general | solution.py:22
  726.3 47.8 %fusion.15 = bf16[1280,4864]{1,0:T(8,128)(2,1)} fusion(f32[2048,4864]{1,0:T(8,128)} %fusion.34, f32[2048,4864]{1,0:T(8,128)} %get-tuple-element.31, bf16[2048,4864]{1,0:T(8,128)(2,1)} %convolution_convert_fusion, bf16[1,2048,1280]{1,2,0:T(8,128)(2,1)} %copy.20, f32[2048]{0:T(1024)S(1)} %copy-done.12), kind=kOutput, calls=%fused_computation.24 | convolution fusion | flops 25625034752 | bytes 117317632 | tf_op jit(solution)/shard_map/transpose(jvp())/dot_general | solution.py:21
  774.1 33.2 %convolution_convert_fusion.3 = bf16[1280,4864]{1,0:T(8,128)(2,1)} fusion(bf16[2048,4864]{1,0:T(8,128)(2,1)} %get-tuple-element.34, bf16[2048,1280]{0,1:T(8,128)(2,1)} %get-tuple-element.33, f32[2048]{0:T(1024)S(1)} %copy-done.8), kind=kOutput, calls=%fused_computation.31 | convolution fusion | flops 25509232640 | bytes 37625856 | tf_op jit(solution)/shard_map/transpose(jvp())/dot_general | solution.py:21
  807.5 77.3 %reduce-scatter.11.cloned.1.call-done = bf16[40,4864]{1,0:T(8,128)(2,1)} async-done(((bf16[1280,4864]{1,0:T(8,128)(2,1)}), bf16[40,4864]{1,0:T(8,128)(2,1)}) %reduce-scatter.11.cloned.1.call-update) | async-done | bytes 389136 | tf_op jit(solution)/shard_map/reduce_scatter | solution.py:43
  884.8 105.3 %reduce-scatter.13.cloned.1.call-done = bf16[40,4864]{1,0:T(8,128)(2,1)} async-done(((bf16[1280,4864]{1,0:T(8,128)(2,1)}), bf16[40,4864]{1,0:T(8,128)(2,1)}) %reduce-scatter.13.cloned.1.call-update) | async-done | bytes 389136 | tf_op jit(solution)/shard_map/reduce_scatter | solution.py:43
  990.1 105.5 %reduce-scatter.7.cloned.1.call-done = bf16[40,4864]{1,0:T(8,128)(2,1)} async-done(((bf16[1280,4864]{1,0:T(8,128)(2,1)}), bf16[40,4864]{1,0:T(8,128)(2,1)}) %reduce-scatter.7.cloned.1.call-update) | async-done | bytes 389136 | tf_op jit(solution)/shard_map/reduce_scatter | solution.py:43
  1095.6 105.3 %reduce-scatter.9.cloned.1.call-done = bf16[40,4864]{1,0:T(8,128)(2,1)} async-done(((bf16[1280,4864]{1,0:T(8,128)(2,1)}), bf16[40,4864]{1,0:T(8,128)(2,1)}) %reduce-scatter.9.cloned.1.call-update) | async-done | bytes 389136 | tf_op jit(solution)/shard_map/reduce_scatter | solution.py:43
  1201.0 66.1 %all-reduce.3.cloned.1.call-done = (bf16[1,40,4864]{2,1,0:T(8,128)(2,1)}, bf16[1,40,4864]{2,1,0:T(8,128)(2,1)}, bf16[1,40,4864]{2,1,0:T(8,128)(2,1)}, bf16[1,40,...) async-done(((bf16[1,40,4864]{2,1,0:T(8,128)(2,1)}, bf16[1,40,4864]{2,1,0:T(8,128)(2,1)}, bf16[1,40,4864]{2,1,0:T(8,128)(2,1)}, ...) | async-done | bytes 2334736 | tf_op jit(solution)/shard_map/psum | solution.py:43
  1275.4 63.6 %psum.55 = f32[]{:T(128)} all-reduce(f32[]{:T(128)S(6)} %add.111), channel_id=1, replica_groups=mesh['rep'=1,'r'=4,'s'=32] {'s'}, use_global_device_ids=true, to_apply=%region_18.19 | all-reduce | flops 1 | bytes 8 | tf_op jit(solution)/shard_map/psum | solution.py:58
  (72 shorter events, 121.8 us)
Async XLA Ops:
  7.2 69.6 %all-gather.13.cloned.1.call-start = ((), (), s32[]{:S(2)}) async-start(), calls=%async_computation.12 | async-start | bytes 12840960 | tf_op jit(solution)/shard_map/all_gather | solution.py:40
  9.3 132.1 %all-gather.15.cloned.1.call-start = ((), (), s32[]{:S(2)}) async-start(), calls=%async_computation.13 | async-start | bytes 12840960 | tf_op jit(solution)/shard_map/all_gather | solution.py:40
  11.4 194.6 %all-gather.17.cloned.1.call-start = ((), (), s32[]{:S(2)}) async-start(), calls=%async_computation.14 | async-start | bytes 12840960 | tf_op jit(solution)/shard_map/all_gather | solution.py:40
  13.5 256.9 %all-gather.21.cloned.1.call-start = ((), (), s32[]{:S(2)}) async-start(), calls=%async_computation.16 | async-start | bytes 12840960 | tf_op jit(solution)/shard_map/all_gather | solution.py:40
  14.1 320.8 %all-gather.23.cloned.1.call-start = ((), (), s32[]{:S(2)}) async-start(), calls=%async_computation.17 | async-start | bytes 12840960 | tf_op jit(solution)/shard_map/all_gather | solution.py:40
  14.7 384.6 %all-gather.19.cloned.1.call-start = ((), (), s32[]{:S(2)}) async-start(), calls=%async_computation.15 | async-start | bytes 12840960 | tf_op jit(solution)/shard_map/all_gather | solution.py:40
  15.3 792.2 %reduce-scatter.15.cloned.1.call-start = ((), (), s32[]{:S(2)}) async-start(), calls=%async_computation.10 | async-start | bytes 12840960 | tf_op jit(solution)/shard_map/reduce_scatter | solution.py:43
  26.9 114.5 %copy-start.11 = (f32[2048]{0:T(1024)}, f32[2048]{0:T(1024)S(1)}, u32[]{:S(2)}) copy-start(f32[2048]{0:T(1024)S(1)} %add_rsqrt_fusion) | copy-start | bytes 24580
  252.6 146.7 %copy-start.6 = (f32[2048]{0:T(1024)}, f32[2048]{0:T(1024)S(1)}, u32[]{:S(2)}) copy-start(f32[2048]{0:T(1024)S(1)} %fusion.91) | copy-start | bytes 24580
  491.9 36.1 %copy-start.10 = (f32[2048]{0:T(1024)S(1)}, f32[2048]{0:T(1024)}, u32[]{:S(2)}) copy-start(f32[2048]{0:T(1024)} %copy-done.9) | copy-start | bytes 24580
  491.9 36.1 %copy-start.7 = (f32[2048]{0:T(1024)S(1)}, f32[2048]{0:T(1024)}, u32[]{:S(2)}) copy-start(f32[2048]{0:T(1024)} %copy-done.6) | copy-start | bytes 24580
  574.1 233.4 %reduce-scatter.17.cloned.1.call-start = ((), (), s32[]{:S(2)}) async-start(), calls=%async_computation.11 | async-start | bytes 12840960 | tf_op jit(solution)/shard_map/reduce_scatter | solution.py:43
  615.8 34.1 %copy-start.12 = (f32[2048]{0:T(1024)S(1)}, f32[2048]{0:T(1024)}, u32[]{:S(2)}) copy-start(f32[2048]{0:T(1024)} %copy-done.11) | copy-start | bytes 24580
  615.8 269.0 %reduce-scatter.11.cloned.1.call-start = ((), (), s32[]{:S(2)}) async-start(), calls=%async_computation.8 | async-start | bytes 12840960 | tf_op jit(solution)/shard_map/reduce_scatter | solution.py:43
  687.7 302.4 %reduce-scatter.13.cloned.1.call-start = ((), (), s32[]{:S(2)}) async-start(), calls=%async_computation.9 | async-start | bytes 12840960 | tf_op jit(solution)/shard_map/reduce_scatter | solution.py:43
  726.2 369.4 %reduce-scatter.7.cloned.1.call-start = ((), (), s32[]{:S(2)}) async-start(), calls=%async_computation.6 | async-start | bytes 12840960 | tf_op jit(solution)/shard_map/reduce_scatter | solution.py:43
  774.1 426.9 %reduce-scatter.9.cloned.1.call-start = ((), (), s32[]{:S(2)}) async-start(), calls=%async_computation.7 | async-start | bytes 12840960 | tf_op jit(solution)/shard_map/reduce_scatter | solution.py:43
  807.3 532.4 %copy-start = (bf16[2,152,1280]{2,1,0:T(8,128)(2,1)S(1)}, bf16[2,152,1280]{2,1,0:T(8,128)(2,1)}, u32[]{:S(2)}) copy-start(bf16[2,152,1280]{2,1,0:T(8,128)(2,1)} %param.15) | copy-start | bytes 2334724
  807.4 536.9 %copy-start.1 = (bf16[2,40,4864]{2,1,0:T(8,128)(2,1)S(1)}, bf16[2,40,4864]{2,1,0:T(8,128)(2,1)}, u32[]{:S(2)}) copy-start(bf16[2,40,4864]{2,1,0:T(8,128)(2,1)} %param.13) | copy-start | bytes 2334724
  807.4 536.9 %copy-start.2 = (bf16[2,40,4864]{2,1,0:T(8,128)(2,1)S(1)}, bf16[2,40,4864]{2,1,0:T(8,128)(2,1)}, u32[]{:S(2)}) copy-start(bf16[2,40,4864]{2,1,0:T(8,128)(2,1)} %param.14) | copy-start | bytes 2334724
  807.4 459.7 %all-reduce.3.cloned.1.call-start = ((), (), s32[]{:S(2)}) async-start(), calls=%async_computation.18 | async-start | bytes 4669440 | tf_op jit(solution)/shard_map/psum | solution.py:43
  1267.0 77.2 %copy-start.3 = (bf16[1,40,4864]{2,1,0:T(8,128)(2,1)S(1)}, bf16[1,40,4864]{2,1,0:T(8,128)(2,1)}, u32[]{:S(2)}) copy-start(bf16[1,40,4864]{2,1,0:T(8,128)(2,1)} %get-tuple-element.9) | copy-start | bytes 1167364
  1267.0 77.2 %copy-start.4 = (bf16[1,40,4864]{2,1,0:T(8,128)(2,1)S(1)}, bf16[1,40,4864]{2,1,0:T(8,128)(2,1)}, u32[]{:S(2)}) copy-start(bf16[1,40,4864]{2,1,0:T(8,128)(2,1)} %get-tuple-element.10) | copy-start | bytes 1167364
  1267.0 77.2 %copy-start.5 = (bf16[1,40,4864]{2,1,0:T(8,128)(2,1)S(1)}, bf16[1,40,4864]{2,1,0:T(8,128)(2,1)}, u32[]{:S(2)}) copy-start(bf16[1,40,4864]{2,1,0:T(8,128)(2,1)} %get-tuple-element.11) | copy-start | bytes 1167364
  (2 other events, 1.3 us)
Sparse Core Ops, SparseCore 0:
  10.9 65.8 all-gather.12
  79.7 61.6 all-gather.14
  144.3 61.6 all-gather.16
  208.7 61.6 all-gather.20
  273.1 61.6 all-gather.22
  337.6 61.6 all-gather.18
  574.2 99.5 reduce-scatter.14
  677.7 101.5 reduce-scatter.16
  783.2 101.5 reduce-scatter.10
  888.5 101.5 reduce-scatter.12
  994.0 101.5 reduce-scatter.6
  1099.4 101.5 reduce-scatter.8
  1203.7 63.2 all-reduce.2
where the time goes:
time: 1370 us; the launch traced here: 1360 us
  waiting for transfers between devices  628 us (46%)
  matrix products  592 us (43%)
  blocking collectives  63.6 us (5%)
  other arithmetic  32.2 us (2%)
  local copies, waits for them, and re-layouts  23.3 us (2%)
  between operations  17.2 us (1%)
    reduce_scatter x6, waiting for transfers between devices, summed(): lax.psum_scatter(term, 's', scatter_dimension=0, tiled=True)  394 us
    dot_general x5, matrix products, layer(): gate = jnp.dot(a, w['w_gate'], preferred_element_type=jnp.float32)  207 us
    dot_general x5, matrix products, layer(): up = jnp.dot(a, w['w_up'], preferred_element_type=jnp.float32)  196 us
    dot_general x5, matrix products, matmul(): jnp.dot(a, w, preferred_element_type=jnp.float32).astype(jnp.bfloat16)  190 us
    all_gather x6, waiting for transfers between devices, fetched(): lax.all_gather(w[number], 's', axis=0, tiled=True)  166 us
    psum x1, waiting for transfers between devices, summed(): lax.psum(lax.psum_scatter(term, 's', scatter_dimension=0, tiled=True), 'r')  66.1 us
    psum x1, blocking collectives, step(): squares = lax.psum(sum((jnp.sum(g * g) for g in gradients)), 's')  63.6 us
  transfers between devices with their start and end apart: 13, of which 11 were waited for; matrix products, arithmetic and copies ran while one was open for 33% of the time, Pallas kernels for 0%

commit v1 on v0

v1 whole, which is shorter than its diff:
```python
import functools

import jax
import jax.numpy as jnp
from jax import lax
from jax.experimental import pallas as pl
from jax.experimental.pallas import tpu as pltpu
from jax.sharding import PartitionSpec as P

NAMES = ("w_gate", "w_up", "w_down")
BF, F32 = jnp.bfloat16, jnp.float32
MESH = pl.DeviceIdType.MESH

TOKENS, D, FF = 2048, 1280, 4864
NY = NZ = NX = 4
S = NY * NZ * 2
RD, RF = D // S, FF // S
TF = 256
NT = FF // TF
ND = D // TF
VMEM_LIMIT = 67_000_000


def dot(a, b, ca, cb):
    return lax.dot_general(a, b, (((ca,), (cb,)), ((), ())), preferred_element_type=F32)


def at(*index):
    return index


def above(i):
    return i * ((i + 64) // 64)


def upto(i, last):
    return last - above(last - i)


def cols(start, size):
    return pl.ds(pl.multiple_of(start, 128), size)


class Place:
    def __init__(self):
        s = lax.axis_index("s")
        self.y, self.z, self.c = lax.div(s, NZ * 2), lax.rem(lax.div(s, 2), NZ), lax.rem(s, 2)
        self.x = lax.axis_index("r")
        self.pos = (self.y, self.z)

    def ring(self, axis, by):
        return lax.rem(self.pos[axis] + by, 4)

    def near(self, axis, by):
        y, z = (self.ring(0, by), self.z) if axis == 0 else (self.y, self.ring(1, by))
        return {"s": (y * NZ + z) * 2 + self.c}

    def partner(self):
        return {"s": (self.y * NZ + self.z) * 2 + 1 - self.c}

    def across(self, by):
        return {"r": lax.rem(self.x + by, NX)}

    def meet(self, x_too):
        barrier = pltpu.get_barrier_semaphore()
        peers = [self.near(axis, by) for axis in (0, 1) for by in (1, 3)] + [self.partner()]
        if x_too:
            peers += [self.across(by) for by in (1, 2, 3)]
        for peer in peers:
            pl.semaphore_signal(barrier, inc=1, device_id=peer, device_id_type=MESH)
        pl.semaphore_wait(barrier, len(peers))


def wait_bytes(ref, sem):
    pltpu.make_async_copy(ref, ref, sem).wait()


CH = NT + ND
LAG = 2
LEAD = 5 * LAG + 1


def gather_kernel(a, wgu, wd, g_gu, g_d, act, gate, up, wt, ssem, rsem, lsem, osem):
    step = pl.program_id(0)
    i = step - LEAD
    me = Place()
    own = [
        pltpu.make_async_copy(wgu, g_gu.at[:, me.y, me.z, me.c], osem.at[0]),
        pltpu.make_async_copy(wd, g_d.at[me.y, me.z, me.c], osem.at[1]),
    ]

    @pl.when(step == 0)
    def _():
        me.meet(False)
        for copy in own:
            copy.start()

    @pl.when(step == 2 * LAG)
    def _():
        for copy in own:
            copy.wait()

    def block(kind, t, half, sub, y, z, c):
        width = TF if half is None else TF // 2
        start = t * TF + (half or 0) * (TF // 2)
        if kind == "gu":
            lead = slice(None) if sub is None else sub
            return g_gu.at[lead, y, z, c, :, cols(start, width)]
        rows = {None: slice(None), 0: pl.ds(0, 80), 1: pl.ds(80, RF - 80)}[sub]
        return g_d.at[y, z, c, rows, cols(start, width)]

    def mine(kind, t, half):
        start = t * TF + half * (TF // 2)
        return wgu.at[:, :, cols(start, TF // 2)] if kind == "gu" else wd.at[:, cols(start, TF // 2)]

    ALL = slice(None)

    def totals(kind, t, k):
        c = me.c
        y, z = [(pl.ds(0, 2), 0), (pl.ds(0, 1), 0), (ALL, pl.ds(0, 2)), (ALL, pl.ds(0, 1)), (ALL, ALL)][k]
        return block(kind, t, None, None, y, z, c)

    def send(kind, t, ch, k):
        def go(src, dst, peer):
            pltpu.make_async_remote_copy(
                src_ref=src, dst_ref=dst, send_sem=ssem.at[k, ch], recv_sem=rsem.at[k, ch], device_id=peer, device_id_type=MESH
            ).start()

        y, z, c = me.y, me.z, me.c
        for half in (0, 1):
            first, second = (0, 1) if half == 0 else (1, 0)
            if k == 0:
                for by in (1, 3):
                    go(mine(kind, t, half), block(kind, t, half, None, y, z, c), me.near(first, by))
            if k == 1:
                for sub, by in ((0, 1), (1, 3)):
                    back = me.ring(first, 4 - by)
                    ref = block(kind, t, half, sub, *((back, z) if first == 0 else (y, back)), c)
                    go(ref, ref, me.near(first, by))
            if k == 2:
                ref = block(kind, t, half, None, *((ALL, z) if first == 0 else (y, ALL)), c)
                for by in (1, 3):
                    go(ref, ref, me.near(second, by))
            if k == 3:
                for sub, by in ((0, 1), (1, 3)):
                    back = me.ring(second, 4 - by)
                    ref = block(kind, t, half, sub, *((ALL, back) if second == 1 else (back, ALL)), c)
                    go(ref, ref, me.near(second, by))
        if k == 4:
            ref = block(kind, t, None, None, ALL, ALL, c)
            go(ref, ref, me.partner())

    def load(t):
        return pltpu.make_async_copy(g_gu.at[:, :, :, :, :, cols(t * TF, TF)], wt.at[lax.rem(t, 2)], lsem.at[lax.rem(t, 2)])

    for k in (5, 4, 3, 2, 1, 0):
        ch = i + 1 + (5 - k) * LAG
        for kind, low, high in (("gu", 0, NT), ("d", NT, CH)):

            @pl.when((ch >= low) & (ch < high))
            def _(k=k, kind=kind, t=ch - low, ch=ch):
                if k > 0:
                    wait_bytes(totals(kind, t, k - 1), rsem.at[k - 1, ch])
                if k < 5:
                    send(kind, t, ch, k)
                elif kind == "gu":
                    load(t).start()

    @pl.when((i >= 0) & (i < NT))
    def _():
        load(i).wait()
        slot = lax.rem(i, 2)
        rows = TOKENS // 4
        for r in range(4):
            part = pl.ds(r * rows, rows)
            g = dot(a[part, :], wt[slot, 0].reshape(D, TF), 1, 0)
            u = dot(a[part, :], wt[slot, 1].reshape(D, TF), 1, 0)
            gate[part, :] = g
            up[part, :] = u
            act[part, :] = (g * jax.nn.sigmoid(g) * u).astype(BF)

    @pl.when(step == LEAD + CH - 2)
    def _():
        for k in range(5):
            for kind, low, high in (("gu", 0, NT), ("d", NT, CH)):

                @pl.loop(low, high)
                def _(ch, k=k, kind=kind, low=low):
                    wait_bytes(totals(kind, ch - low, k), ssem.at[k, ch])


def gathered(a, wgu, wd, number):
    tile = pl.BlockSpec((TOKENS, TF), lambda step: (0, upto(above(step - LEAD), NT - 1)))
    vmem, hbm = pl.BlockSpec(memory_space=pltpu.VMEM), pl.BlockSpec(memory_space=pl.ANY)
    g_gu, g_d, *rest = pl.pallas_call(
        gather_kernel,
        grid=(LEAD + CH - 1,),
        in_specs=[vmem, vmem, vmem],
        out_specs=[hbm, hbm, tile, tile, tile],
        out_shape=[
            jax.ShapeDtypeStruct((2, NY, NZ, 2, RD, FF), BF),
            jax.ShapeDtypeStruct((NY, NZ, 2, RF, D), BF),
            jax.ShapeDtypeStruct((TOKENS, FF), BF),
            jax.ShapeDtypeStruct((TOKENS, FF), F32),
            jax.ShapeDtypeStruct((TOKENS, FF), F32),
        ],
        scratch_shapes=[
            pltpu.VMEM((2, 2, NY, NZ, 2, RD, TF), BF),
            pltpu.SemaphoreType.DMA((5, CH)),
            pltpu.SemaphoreType.DMA((5, CH)),
            pltpu.SemaphoreType.DMA((2,)),
            pltpu.SemaphoreType.DMA((2,)),
        ],
        compiler_params=pltpu.CompilerParams(
            collective_id=number, has_side_effects=True, vmem_limit_bytes=VMEM_LIMIT, dimension_semantics=("arbitrary",)
        ),
        cost_estimate=pl.CostEstimate(flops=4 * TOKENS * D * FF, bytes_accessed=200_000_000, transcendentals=TOKENS * FF),
        name=f"gather_{number}",
    )(a, wgu, wd)
    return g_gu.reshape(2, D, FF), g_d.reshape(FF, D), *rest


DC = 128
NDC = D // DC
TAIL = 7


class Summing:
    HEIGHTS = {"gu": ((RD, RD), (RD, RD)), "d": ((40, 40), (40, RF - 120))}

    def __init__(self, kind, count, entry, me, own, inbox, s1, r2, s2, r3, acc, s4, r4, s5, r5, xb, ssem, rsem, out):
        self.kind, self.count, self.entry, self.me = kind, count, entry, me
        self.own, self.inbox, self.s1, self.r2, self.s2, self.r3 = own, inbox, s1, r2, s2, r3
        self.acc, self.s4, self.r4, self.s5, self.r5, self.xb = acc, s4, r4, s5, r5, xb
        self.ssem, self.rsem, self.out = ssem, rsem, out
        self.subs = (slice(None),) if kind == "gu" else (0, 1)

    def part(self, half, sub):
        if self.kind == "gu":
            return sub, slice(None), pl.ds(half * 128, 128)
        low = 80 * half + 40 * sub
        return 0, pl.ds(low, self.HEIGHTS["d"][half][sub]), slice(None)

    def rows(self, half, sub):
        return slice(None) if self.kind == "gu" else pl.ds(0, self.HEIGHTS["d"][half][sub])

    def both(self, slot, y, z, half, sub):
        lead, rows, columns = self.part(half, sub)
        mine = self.own[slot, lead, y, z, self.me.c, rows, columns] if self.kind == "gu" else self.own[slot, y, z, rows, columns]
        theirs = self.inbox[slot, lead, y, z, rows, columns] if self.kind == "gu" else self.inbox[slot, y, z, rows, columns]
        return mine.astype(F32) + theirs.astype(F32)

    def size(self, k, slot, two):
        if k == 0:
            return self.inbox.at[slot]
        if k == 5:
            return self.xb.at[two, pl.ds(0, 3)]
        if self.kind == "gu":
            return (self.r2, self.r3, self.r4, self.r5)[k - 1].at[two]
        return self.inbox.at[(slot, *((0,), (pl.ds(0, 2),), (0, 0), (0, pl.ds(0, 2)))[k - 1])]

    def compute(self, k, t):
        me, slot, two = self.me, lax.rem(t, 4), lax.rem(t, 2)
        if k > 0:
            wait_bytes(self.size(k - 1, slot, two), self.rsem.at[k - 1, slot])
            wait_bytes(self.size(k - 1, slot, two), self.ssem.at[k - 1, slot])
        if k == 6:
            total = self.xb[two, 0].astype(F32)
            for x in range(1, NX):
                total = total + self.xb[two, x].astype(F32)
            if self.kind == "gu":
                self.out[:, :, cols(t * TF, TF)] = total.astype(BF)
            else:
                self.out[:, cols(t * DC, DC)] = total.astype(BF)
            return
        for half in (0, 1):
            first, second = (0, 1) if half == 0 else (1, 0)
            along = lambda place: (place, slice(None)) if first == 0 else (slice(None), place)
            for sub in (0, 1):
                rows = self.rows(half, sub)
                if k == 1:
                    self.s1[half, sub, :, rows] = self.both(slot, *along(me.ring(first, 2)), half, sub).astype(BF)
                if k == 2:
                    for way, by in ((0, 1), (1, 3)):
                        term = self.both(slot, *along(me.ring(first, by)), half, sub)
                        if sub == way:
                            term = term + self.r2[two, half, sub, :, rows].astype(F32)
                        self.s2[half, way, sub, :, rows] = term.astype(BF)
                if k == 3:
                    term = self.both(slot, *along(me.pos[first]), half, sub)
                    for way in (0, 1):
                        term = term + self.r3[two, half, way, sub, :, rows].astype(F32)
                    self.acc[two, half, sub, :, rows] = term
                    self.s4[half, sub, rows] = self.acc[two, half, sub, me.ring(second, 2), rows].astype(BF)
                if k == 4:
                    for way, by in ((0, 1), (1, 3)):
                        term = self.acc[two, half, sub, me.ring(second, by), rows]
                        if sub == way:
                            term = term + self.r4[two, half, sub, rows].astype(F32)
                        self.s5[half, way, sub, rows] = term.astype(BF)
                if k == 5:
                    term = self.acc[two, half, sub, me.pos[second], rows]
                    for way in (0, 1):
                        term = term + self.r5[two, half, way, sub, rows].astype(F32)
                    lead, where, columns = self.part(half, sub)
                    if self.kind == "gu":
                        self.xb[two, me.x, lead, where, columns] = term.astype(BF)
                    else:
                        self.xb[two, me.x, where, columns] = term.astype(BF)

    def send(self, k, t, source=None):
        me, slot, two = self.me, lax.rem(t, 4), lax.rem(t, 2)

        def go(src, dst, peer):
            pltpu.make_async_remote_copy(
                src_ref=src, dst_ref=dst, send_sem=self.ssem.at[k, slot], recv_sem=self.rsem.at[k, slot], device_id=peer, device_id_type=MESH
            ).start()

        if k == 0:
            go(source, self.inbox.at[slot], me.partner())
        if k == 5:
            for by in (1, 2, 3):
                go(self.xb.at[two, me.x], self.xb.at[two, me.x], me.across(by))
        for half in (0, 1):
            first, second = (0, 1) if half == 0 else (1, 0)
            for way, by in ((0, 1), (1, 3)):
                if k == 1:
                    rows = self.rows(half, way)
                    go(self.s1.at[half, way, :, rows], self.r2.at[two, half, way, :, rows], me.near(first, by))
                if k == 3:
                    rows = self.rows(half, way)
                    go(self.s4.at[half, way, rows], self.r4.at[two, half, way, rows], me.near(second, by))
                if k in (2, 4):
                    for sub in self.subs:
                        rows = self.rows(half, sub)
                        if k == 2:
                            go(self.s2.at[half, way, sub, :, rows], self.r3.at[two, half, way, sub, :, rows], me.near(first, by))
                        else:
                            go(self.s5.at[half, way, sub, rows], self.r5.at[two, half, way, sub, rows], me.near(second, by))


def stage_buffers(kind):
    block = (2, NY, NZ, RD, TF) if kind == "gu" else (NY, NZ, RF, DC)
    last = (2, RD, TF) if kind == "gu" else (RF, DC)
    return [
        pltpu.VMEM((4, 2, NY, NZ, 2, RD, TF) if kind == "gu" else (4, *block), BF),
        pltpu.VMEM((4, *block), BF),
        pltpu.VMEM((2, 2, 4, 40, 128), BF),
        pltpu.VMEM((2, 2, 2, 4, 40, 128), BF),
        pltpu.VMEM((2, 2, 2, 4, 40, 128), BF),
        pltpu.VMEM((2, 2, 2, 2, 4, 40, 128), BF),
        pltpu.VMEM((2, 2, 2, 4, 40, 128), F32),
        pltpu.VMEM((2, 2, 40, 128), BF),
        pltpu.VMEM((2, 2, 2, 40, 128), BF),
        pltpu.VMEM((2, 2, 2, 40, 128), BF),
        pltpu.VMEM((2, 2, 2, 2, 40, 128), BF),
        pltpu.VMEM((2, NX, *last), BF),
        pltpu.SemaphoreType.DMA((6, 4)),
        pltpu.SemaphoreType.DMA((6, 4)),
    ]


NBUF = 14


def back_kernel(with_da, *refs):
    refs = list(refs)
    take = lambda n: [refs.pop(0) for _ in range(n)]
    a, dy, wd, gate, up, dwd = take(6)
    wgu = take(1)[0] if with_da else None
    out_gu, out_d = take(2)
    da = take(1)[0] if with_da else None
    gu_bufs, d_bufs = take(NBUF), take(NBUF)
    dg_s, du_s, lsem = take(3)
    i = pl.program_id(0)
    me = Place()

    @pl.when(i == 0)
    def _():
        me.meet(True)

    own = gu_bufs[0]
    gu = Summing("gu", NT, 1, me, *gu_bufs, out_gu)
    down = Summing("d", NDC, 1, me, *d_bufs, out_d)

    def load(n):
        return pltpu.make_async_copy(dwd.at[:, :, me.c, :, cols(n * DC, DC)], down.own.at[lax.rem(n, 4)], lsem.at[lax.rem(n, 4)])

    for k in (6, 5, 4, 3, 2, 1):
        for engine in (gu, down):
            t = i - engine.entry - k

            @pl.when((t >= 0) & (t < engine.count))
            def _(k=k, engine=engine, t=t):
                if k == 1 and engine is down:
                    load(t).wait()
                engine.compute(k, t)

    for k in (5, 4, 3, 2, 1, 0):
        for engine in (gu, down):
            t = i - engine.entry - k

            @pl.when((t >= 0) & (t < engine.count))
            def _(k=k, engine=engine, t=t):
                source = None
                if k == 0:
                    source = own.at[lax.rem(t, 4), :, :, :, 1 - me.c] if engine is gu else dwd.at[:, :, 1 - me.c, :, cols(t * DC, DC)]
                engine.send(k, t, source)

    @pl.when(i < NDC)
    def _():
        load(i).start()

    @pl.when(i < NT)
    def _():
        slot = lax.rem(i, 4)
        rows = TOKENS // 4
        for r in range(4):
            part = pl.ds(r * rows, rows)
            dh = dot(dy[part, :], wd[...], 1, 1).astype(BF).astype(F32)
            g, u = gate[part, :], up[part, :]
            sg = jax.nn.sigmoid(g)
            du_s[part, :] = (dh * (g * sg)).astype(BF)
            dg_s[part, :] = (dh * u * (sg * (1 + g * (1 - sg)))).astype(BF)
        own[slot, 0] = dot(a[...], dg_s[...], 0, 0).reshape(NY, NZ, 2, RD, TF).astype(BF)
        own[slot, 1] = dot(a[...], du_s[...], 0, 0).reshape(NY, NZ, 2, RD, TF).astype(BF)
        if with_da:
            for r in range(4):
                part = pl.ds(r * rows, rows)
                more = dot(dg_s[part, :], wgu[0], 1, 1) + dot(du_s[part, :], wgu[1], 1, 1)

                @pl.when(i == 0)
                def _():
                    da[part, :] = more

                @pl.when(i > 0)
                def _():
                    da[part, :] += more


def backward(a, dy, g_d, gate, up, dwd, g_gu, number):
    with_da = g_gu is not None
    last = lambda i: upto(i, NT - 1)
    vmem, hbm = pl.BlockSpec(memory_space=pltpu.VMEM), pl.BlockSpec(memory_space=pl.ANY)
    tile = pl.BlockSpec((TOKENS, TF), lambda i: (0, last(i)))
    in_specs = [vmem, vmem, pl.BlockSpec((TF, D), lambda i: (last(i), 0)), tile, tile, hbm]
    out_shape = [jax.ShapeDtypeStruct((2, RD, FF), BF), jax.ShapeDtypeStruct((RF, D), BF)]
    operands = [a, dy, g_d, gate, up, dwd.reshape(NY, NZ, 2, RF, D)]
    if with_da:
        in_specs.append(pl.BlockSpec((2, D, TF), lambda i: (0, 0, last(i))))
        out_shape.append(jax.ShapeDtypeStruct((TOKENS, D), F32))
        operands.append(g_gu)
    return pl.pallas_call(
        functools.partial(back_kernel, with_da),
        grid=(NT + TAIL,),
        in_specs=in_specs,
        out_specs=[vmem] * len(out_shape),
        out_shape=out_shape,
        scratch_shapes=[
            *stage_buffers("gu"),
            *stage_buffers("d"),
            pltpu.VMEM((TOKENS, TF), BF),
            pltpu.VMEM((TOKENS, TF), BF),
            pltpu.SemaphoreType.DMA((4,)),
        ],
        compiler_params=pltpu.CompilerParams(
            collective_id=number, has_side_effects=True, vmem_limit_bytes=VMEM_LIMIT, dimension_semantics=("arbitrary",)
        ),
        cost_estimate=pl.CostEstimate(
            flops=(10 if with_da else 6) * TOKENS * D * FF, bytes_accessed=200_000_000, transcendentals=TOKENS * FF
        ),
        name=f"backward_{number}",
    )(*operands)


def total_kernel(part, out, b0, b1, b2, ssem, rsem):
    me = Place()
    barrier = pltpu.get_barrier_semaphore()
    rings = [[me.near(axis, by) for by in (1, 2, 3)] for axis in (0, 1)] + [[me.partner()]]
    peers = [peer for ring in rings for peer in ring]
    for peer in peers:
        pl.semaphore_signal(barrier, inc=1, device_id=peer, device_id_type=MESH)
    pl.semaphore_wait(barrier, len(peers))
    value = part[...]
    for k, (buf, place, ring) in enumerate(zip((b0, b1, b2), (me.y, me.z, me.c), rings, strict=True)):
        buf[place] = value
        for peer in ring:
            pltpu.make_async_remote_copy(
                src_ref=buf.at[place], dst_ref=buf.at[place], send_sem=ssem.at[k], recv_sem=rsem.at[k], device_id=peer, device_id_type=MESH
            ).start()
        wait_bytes(buf.at[pl.ds(0, len(ring))], rsem.at[k])
        wait_bytes(buf.at[pl.ds(0, len(ring))], ssem.at[k])
        value = buf[0]
        for n in range(1, len(ring) + 1):
            value = value + buf[n]
    out[...] = value


def over_group(number, collective):
    part = jnp.full((8, 128), number, F32)
    vmem = pl.BlockSpec(memory_space=pltpu.VMEM)
    out = pl.pallas_call(
        total_kernel,
        in_specs=[vmem],
        out_specs=vmem,
        out_shape=jax.ShapeDtypeStruct((8, 128), F32),
        scratch_shapes=[
            pltpu.VMEM((NY, 8, 128), F32),
            pltpu.VMEM((NZ, 8, 128), F32),
            pltpu.VMEM((2, 8, 128), F32),
            pltpu.SemaphoreType.DMA((3,)),
            pltpu.SemaphoreType.DMA((3,)),
        ],
        compiler_params=pltpu.CompilerParams(collective_id=collective, has_side_effects=True),
        name="total",
    )(part)
    return out[0, 0]


def normed(h):
    wide = h.astype(F32)
    scale = lax.rsqrt(jnp.mean(wide**2, -1, keepdims=True) + 1e-6)
    return (wide * scale).astype(BF)


def adamw(w, m, v, g):
    m = 0.9 * m + 0.1 * g
    v = 0.95 * v + 0.05 * g * g
    step = m * lax.rsqrt(v + 1e-8) + 0.1 * w
    return (w - 0.02 * step).astype(BF), m, v


def clipped(gradients, sum_of_squares, count):
    factor = jnp.minimum(1.0, 0.5 * lax.rsqrt(sum_of_squares / count + 1e-30))
    return [g * factor for g in gradients]


def solution(mesh):
    def step(x, dy, *arrays):
        weights, m, v = (arrays[i : i + 3] for i in (0, 3, 6))
        shards = lambda layer: (jnp.stack([weights[0][layer], weights[1][layer]]), weights[2][layer])
        h0, dy = x[0], dy[0]
        a0 = normed(h0)
        gu0, d0, act0, gate0, up0 = gathered(a0, *shards(0), 0)
        h1 = h0 + dot(act0, d0, 1, 0).astype(BF)
        a1, back = jax.vjp(normed, h1)
        gu1, d1, act1, gate1, up1 = gathered(a1, *shards(1), 1)
        by_d1 = dot(act1, dy, 0, 0).astype(BF)
        mine_gu1, mine_d1, da = backward(a1, dy, d1, gate1, up1, by_d1, gu1, 2)
        dh = dy + back(da.astype(BF))[0]
        by_d0 = dot(act0, dh, 0, 0).astype(BF)
        mine_gu0, mine_d0 = backward(a0, dh, d0, gate0, up0, by_d0, None, 3)
        gradients = [jnp.stack([mine_gu0[n], mine_gu1[n]]).astype(F32) for n in (0, 1)] + [jnp.stack([mine_d0, mine_d1]).astype(F32)]
        squares = over_group(sum(jnp.sum(g * g) for g in gradients), 4)
        gradients = clipped(gradients, squares, S * sum(g.size for g in gradients))
        new = [adamw(w.astype(F32), m, v, g) for w, m, v, g in zip(weights, m, v, gradients, strict=True)]
        return tuple(one[which] for which in range(3) for one in new)

    states, cut = P(("rep", "r", "s"), None, None), P(None, "s", None)
    return jax.shard_map(
        step,
        mesh=mesh,
        in_specs=(states, states) + (cut,) * 9,
        out_specs=(P("rep", "s", None),) * 9,
        check_vma=False,
    )
```

time: 1370 us -> 806 us (0.59)
  Pallas kernels: 0 us -> 647 us
  waiting for transfers between devices: 628 us -> 0 us
  matrix products: 592 us -> 102 us
  blocking collectives: 63.6 us -> 0 us
    pallas_call x0 -> x5, Pallas kernels: none -> 647 us  [the longest x2 394 us: backward(): pl.pallas_call(functools.partial(back_kernel, with_da), grid=(NT + TAIL,)...]
    dot_general x15 -> x3, matrix products: 592 us -> 102 us  [dot(): lax.dot_general(a, b, (((ca,), (cb,)), ((), ())), preferred_element_type=...]
    reduce_scatter x6 -> x0, waiting for transfers between devices: 394 us -> none  [summed(): lax.psum_scatter(term, 's', scatter_dimension=0, tiled=True)]
    all_gather x6 -> x0, waiting for transfers between devices: 166 us -> none  [fetched(): lax.all_gather(w[number], 's', axis=0, tiled=True)]
    psum x1 -> x0, waiting for transfers between devices: 66.1 us -> none  [summed(): lax.psum(lax.psum_scatter(term, 's', scatter_dimension=0, tiled=True), 'r')]
    psum x1 -> x0, blocking collectives: 63.6 us -> none  [step(): squares = lax.psum(sum((jnp.sum(g * g) for g in gradients)), 's')]
  transfers between devices with their start and end apart: 13 -> 0, of which waited for: 11 -> 0; matrix products, arithmetic and copies ran while one was open for 33% -> 0% of each run, Pallas kernels for 0% -> 0%
where the time goes in v1:
time: 806 us; the launch traced here: 803 us
  Pallas kernels  647 us (80%)
  matrix products  102 us (13%)
  other arithmetic  37.4 us (5%)
  local copies, waits for them, and re-layouts  13.1 us (2%)
    pallas_call x2, Pallas kernels, backward(): pl.pallas_call(functools.partial(back_kernel, with_da), grid=(NT + TAIL,)...  394 us
    pallas_call x2, Pallas kernels, gathered(): pl.pallas_call(gather_kernel, grid=(LEAD + CH - 1,), in_specs=[vmem, vmem...  235 us
    dot_general x3, matrix products, dot(): lax.dot_general(a, b, (((ca,), (cb,)), ((), ())), preferred_element_type=...  102 us
    pallas_call x1, Pallas kernels, over_group(): pl.pallas_call(total_kernel, in_specs=[vmem], out_specs=vmem, out_shape=j...  17.8 us

profile of v1, /device:TPU:1, one launch (start us, length us, event | category | flops | bytes accessed | tf_op | source)
XLA Modules:
  0.0 803.2 jit_solution(2802153813066070631)
XLA Ops:
  0.7 3.7 fusion
  5.6 1.3 pad_maximum_fusion
  7.8 3.3 fusion.1.a.refs_0_
  11.1 120.2 %gather_0.1 = (bf16[2,4,4,2,40,4864]{5,4,3,2,1,0:T(8,128)(2,1)}, bf16[4,4,2,152,1280]{4,3,2,1,0:T(8,128)(2,1)}, bf16[2048,4864]{1,0:T(8,128)(2,1)}, f32[2048,4864]{1,0:T(8,128)}, f32[2048,4864]{1,0:T(8,128)}) custom-call(bf16[2048,1280]{1,0:T(8,128)(2,1)} %fusion.1.a.refs_0_, bf16[2,40,4864]{2,1,0:T(8,128)(2,1)} %get-tuple-element.58.wgu, ...), custom_call_target="tpu_custom_call" | custom-call | flops 51002736640 | bytes 200000000 | tf_op jit(solution)/shard_map/gather_0/pallas_call | solution.py:195
  131.3 33.3 %fusion.4 = (f32[2048]{0:T(1024)S(1)}, bf16[2048,1280]{1,0:T(8,128)(2,1)S(1)}) fusion(bf16[2048,4864]{1,0:T(8,128)(2,1)} %get-tuple-element.23, bf16[4864,1280]{1,0:T(8,128)(2,1)} %bitcast.33, bf16[1,2048,1280]{2,1,0:T(8,128)(2,1)} %param.11), kind=kOutput, calls=%fused_computation.13 | convolution fusion | flops 25514473472 | bytes 42868736 | tf_op jit(solution)/shard_map/dot_general | solution.py:25
  165.2 1.7 copy-done
  167.5 3.2 fusion.5.a.refs_0_
  170.7 115.1 %gather_1.1 = (bf16[2,4,4,2,40,4864]{5,4,3,2,1,0:T(8,128)(2,1)}, bf16[4,4,2,152,1280]{4,3,2,1,0:T(8,128)(2,1)}, bf16[2048,4864]{1,0:T(8,128)(2,1)}, f32[2048,4864]{1,0:T(8,128)}, f32[2048,4864]{1,0:T(8,128)}) custom-call(bf16[2048,1280]{1,0:T(8,128)(2,1)} %fusion.5.a.refs_0_, bf16[2,40,4864]{2,1,0:T(8,128)(2,1)} %get-tuple-element.59.wgu, ...), custom_call_target="tpu_custom_call" | custom-call | flops 51002736640 | bytes 200000000 | tf_op jit(solution)/shard_map/gather_1/pallas_call | solution.py:195
  285.8 34.3 %convolution_convert_fusion.1 = bf16[4864,1280]{1,0:T(8,128)(2,1)} fusion(bf16[2048,4864]{1,0:T(8,128)(2,1)} %get-tuple-element.28, bf16[1,2048,1280]{2,1,0:T(8,128)(2,1)} %param.12), kind=kOutput, calls=%fused_computation.1 | convolution fusion | flops 25507594240 | bytes 37617664 | tf_op jit(solution)/shard_map/dot_general | solution.py:25
  320.1 237.9 %backward_2.1 = (bf16[2,40,4864]{2,1,0:T(8,128)(2,1)}, bf16[152,1280]{1,0:T(8,128)(2,1)}, f32[2048,1280]{1,0:T(8,128)}) custom-call(bf16[2048,1280]{1,0:T(8,128)(2,1)} %fusion.5.a.refs_0_, bf16[2048,1280]{1,0:T(8,128)(2,1)} %bitcast.27, bf16[4864,1280]{1,0:T(8,128)(2,1)} %bitcast.35, f32[2048,4864]{1,0:T(8,128)} %get-tuple-element.26.refs_3_, ...), custom_call_target="tpu_custom_call" | custom-call | flops 127506841600 | bytes 200000000 | tf_op jit(solution)/shard_map/backward_2/pallas_call | solution.py:453
  558.0 2.0 fusion.39
  560.1 6.8 fusion.6
  567.1 1.6 copy-done.2
  568.7 5.9 fusion.8.refs_1_
  574.6 34.5 %convolution_convert_fusion = bf16[4864,1280]{1,0:T(8,128)(2,1)} fusion(bf16[2048,4864]{1,0:T(8,128)(2,1)} %get-tuple-element.23, bf16[2048,1280]{1,0:T(8,128)(2,1)S(1)} %fusion.8.refs_1_), kind=kOutput, calls=%fused_computation | convolution fusion | flops 25507594240 | bytes 37617664 | tf_op jit(solution)/shard_map/dot_general | solution.py:25
  609.1 155.9 %backward_3.1 = (bf16[2,40,4864]{2,1,0:T(8,128)(2,1)}, bf16[152,1280]{1,0:T(8,128)(2,1)}) custom-call(bf16[2048,1280]{1,0:T(8,128)(2,1)} %fusion.1.a.refs_0_, bf16[2048,1280]{1,0:T(8,128)(2,1)} %copy-done.3, bf16[4864,1280]{1,0:T(8,128)(2,1)} %bitcast.34, f32[2048,4864]{1,0:T(8,128)} %get-tuple-element.31.refs_3_, f32[2048,4864]{1,0:T(8,128)} %get-tuple-element.32.refs_4_, ...), custom_call_target="tpu_custom_call" | custom-call | flops 76504104960 | bytes 200000000 | tf_op jit(solution)/shard_map/backward_3/pallas_call | solution.py:453
  765.0 2.2 fusion.20
  767.2 1.3 fusion.38
  773.0 17.8 %total.1 = f32[8,128]{1,0:T(8,128)} custom-call(f32[8,128]{1,0:T(8,128)} %broadcast_in_dim.2.part), custom_call_target="tpu_custom_call" | custom-call | tf_op jit(solution)/shard_map/total/pallas_call | solution.py:502
  790.8 1.2 slice.43
  792.8 4.3 fusion.26
  797.2 2.3 fusion.17
  799.6 1.1 copy-done.17
  800.7 2.3 fusion.23
  (55 shorter events, 6.2 us)
Async XLA Ops:
  0.6 3.8 copy-start.8
  0.7 7.2 slice-start
  4.4 1.1 copy-start.10
  4.4 3.4 slice-start.1
  5.6 1.3 copy-start.6
  164.6 0.6 copy-start.20
  164.6 2.3 copy-start
  166.9 0.6 copy-start.18
  560.1 6.8 copy-start.21
  560.1 7.0 copy-start.1
  560.1 8.6 %copy-start.2 = (bf16[1,2048,1280]{2,1,0:T(8,128)(2,1)S(1)}, bf16[1,2048,1280]{2,1,0:T(8,128)(2,1)}, u32[]{:S(2)}) copy-start(bf16[1,2048,1280]{2,1,0:T(8,128)(2,1)} %param.12) | copy-start | bytes 15728644
  560.1 8.6 %copy-start.19 = (f32[2048]{0:T(1024)S(1)}, f32[2048]{0:T(1024)}, u32[]{:S(2)}) copy-start(f32[2048]{0:T(1024)} %copy-done.18) | copy-start | bytes 24580
  574.6 34.5 %copy-start.3 = (bf16[2048,1280]{1,0:T(8,128)(2,1)}, bf16[2048,1280]{1,0:T(8,128)(2,1)S(1)}, u32[]{:S(2)}) copy-start(bf16[2048,1280]{1,0:T(8,128)(2,1)S(1)} %fusion.8.refs_1_) | copy-start | bytes 15728644
  765.0 3.5 copy-start.5
  765.0 4.5 copy-start.4
  767.2 25.6 %copy-start.7 = (bf16[2,152,1280]{2,1,0:T(8,128)(2,1)S(1)}, bf16[2,152,1280]{2,1,0:T(8,128)(2,1)}, u32[]{:S(2)}) copy-start(bf16[2,152,1280]{2,1,0:T(8,128)(2,1)} %param.15) | copy-start | bytes 2334724
  767.2 25.6 %copy-start.12 = (bf16[152,1280]{1,0:T(8,128)(2,1)S(1)}, bf16[152,1280]{1,0:T(8,128)(2,1)}, u32[]{:S(2)}) copy-start(bf16[152,1280]{1,0:T(8,128)(2,1)} %get-tuple-element.36) | copy-start | bytes 1167364
  767.2 25.6 %copy-start.13 = (bf16[152,1280]{1,0:T(8,128)(2,1)S(1)}, bf16[152,1280]{1,0:T(8,128)(2,1)}, u32[]{:S(2)}) copy-start(bf16[152,1280]{1,0:T(8,128)(2,1)} %get-tuple-element.35) | copy-start | bytes 1167364
  792.8 4.4 copy-start.9
  792.8 4.4 copy-start.14
  792.8 4.4 copy-start.15
  797.1 2.4 copy-start.11
  797.2 2.4 copy-start.16
  797.2 3.5 copy-start.17

commit v2 on v1

--- a/solution.py
+++ b/solution.py
@@ -80,7 +80,11 @@
 LEAD = 5 * LAG + 1
 
 
-def gather_kernel(a, wgu, wd, g_gu, g_d, act, gate, up, wt, ssem, rsem, lsem, osem):
+def gather_kernel(forward, *refs):
+    if forward:
+        a, wgu, wd, h, g_gu, g_d, act, gate, up, h_new, wt, wdt, act_s, ssem, rsem, lsem, osem = refs
+    else:
+        a, wgu, wd, dy, g_gu, g_d, gate, up, dwd, wt, act_s, ssem, rsem, lsem, osem = refs
     step = pl.program_id(0)
     i = step - LEAD
     me = Place()
@@ -150,8 +154,11 @@
             ref = block(kind, t, None, None, ALL, ALL, c)
             go(ref, ref, me.partner())
 
-    def load(t):
-        return pltpu.make_async_copy(g_gu.at[:, :, :, :, :, cols(t * TF, TF)], wt.at[lax.rem(t, 2)], lsem.at[lax.rem(t, 2)])
+    def load(kind, t):
+        slot = lax.rem(t, 2)
+        if kind == "gu":
+            return pltpu.make_async_copy(g_gu.at[:, :, :, :, :, cols(t * TF, TF)], wt.at[slot], lsem.at[0, slot])
+        return pltpu.make_async_copy(g_d.at[:, :, :, :, cols(t * TF, TF)], wdt.at[slot], lsem.at[1, slot])
 
     for k in (5, 4, 3, 2, 1, 0):
         ch = i + 1 + (5 - k) * LAG
@@ -163,23 +170,33 @@
                     wait_bytes(totals(kind, t, k - 1), rsem.at[k - 1, ch])
                 if k < 5:
                     send(kind, t, ch, k)
-                elif kind == "gu":
-                    load(t).start()
+                elif kind == "gu" or forward:
+                    load(kind, t).start()
 
     @pl.when((i >= 0) & (i < NT))
     def _():
-        load(i).wait()
+        load("gu", i).wait()
         slot = lax.rem(i, 2)
-        rows = TOKENS // 4
-        for r in range(4):
-            part = pl.ds(r * rows, rows)
-            g = dot(a[part, :], wt[slot, 0].reshape(D, TF), 1, 0)
-            u = dot(a[part, :], wt[slot, 1].reshape(D, TF), 1, 0)
-            gate[part, :] = g
-            up[part, :] = u
-            act[part, :] = (g * jax.nn.sigmoid(g) * u).astype(BF)
-
-    @pl.when(step == LEAD + CH - 2)
+        g = dot(a[...], wt[slot, 0].reshape(D, TF), 1, 0)
+        u = dot(a[...], wt[slot, 1].reshape(D, TF), 1, 0)
+        gate[...] = g
+        up[...] = u
+        hidden = (g * jax.nn.sigmoid(g) * u).astype(BF)
+        if forward:
+            act[...] = hidden
+            act_s[:, cols(i * TF, TF)] = hidden
+        else:
+            act_s[...] = hidden
+            dwd[...] = dot(act_s[...], dy[...], 0, 0).astype(BF)
+
+    if forward:
+
+        @pl.when(i >= NT)
+        def _():
+            load("d", i - NT).wait()
+            h_new[...] = h[...] + dot(act_s[...], wdt[lax.rem(i - NT, 2)].reshape(FF, TF), 1, 0).astype(BF)
+
+    @pl.when(step == LEAD + CH - 1)
     def _():
         for k in range(5):
             for kind, low, high in (("gu", 0, NT), ("d", NT, CH)):
@@ -189,51 +206,60 @@
                     wait_bytes(totals(kind, ch - low, k), ssem.at[k, ch])
 
 
-def gathered(a, wgu, wd, number):
+def gathered(a, wgu, wd, other, number):
+    forward = number == 0
+    vmem, hbm = pl.BlockSpec(memory_space=pltpu.VMEM), pl.BlockSpec(memory_space=pl.ANY)
     tile = pl.BlockSpec((TOKENS, TF), lambda step: (0, upto(above(step - LEAD), NT - 1)))
-    vmem, hbm = pl.BlockSpec(memory_space=pltpu.VMEM), pl.BlockSpec(memory_space=pl.ANY)
+    column = pl.BlockSpec((TOKENS, TF), lambda step: (0, above(step - LEAD - NT)))
+    row = pl.BlockSpec((TF, D), lambda step: (upto(above(step - LEAD), NT - 1), 0))
+    shape = jax.ShapeDtypeStruct
+    wide = [shape((TOKENS, FF), F32)] * 2
     g_gu, g_d, *rest = pl.pallas_call(
-        gather_kernel,
-        grid=(LEAD + CH - 1,),
-        in_specs=[vmem, vmem, vmem],
-        out_specs=[hbm, hbm, tile, tile, tile],
+        functools.partial(gather_kernel, forward),
+        grid=(LEAD + CH,),
+        in_specs=[vmem, vmem, vmem, column if forward else vmem],
+        out_specs=[hbm, hbm, *([tile] * 3 + [column] if forward else [tile, tile, row])],
         out_shape=[
-            jax.ShapeDtypeStruct((2, NY, NZ, 2, RD, FF), BF),
-            jax.ShapeDtypeStruct((NY, NZ, 2, RF, D), BF),
-            jax.ShapeDtypeStruct((TOKENS, FF), BF),
-            jax.ShapeDtypeStruct((TOKENS, FF), F32),
-            jax.ShapeDtypeStruct((TOKENS, FF), F32),
+            shape((2, NY, NZ, 2, RD, FF), BF),
+            shape((NY, NZ, 2, RF, D), BF),
+            *([shape((TOKENS, FF), BF), *wide, shape((TOKENS, D), BF)] if forward else [*wide, shape((FF, D), BF)]),
         ],
         scratch_shapes=[
             pltpu.VMEM((2, 2, NY, NZ, 2, RD, TF), BF),
+            *([pltpu.VMEM((2, NY, NZ, 2, RF, TF), BF), pltpu.VMEM((TOKENS, FF), BF)] if forward else [pltpu.VMEM((TOKENS, TF), BF)]),
             pltpu.SemaphoreType.DMA((5, CH)),
             pltpu.SemaphoreType.DMA((5, CH)),
-            pltpu.SemaphoreType.DMA((2,)),
+            pltpu.SemaphoreType.DMA((2, 2)),
             pltpu.SemaphoreType.DMA((2,)),
         ],
         compiler_params=pltpu.CompilerParams(
             collective_id=number, has_side_effects=True, vmem_limit_bytes=VMEM_LIMIT, dimension_semantics=("arbitrary",)
         ),
-        cost_estimate=pl.CostEstimate(flops=4 * TOKENS * D * FF, bytes_accessed=200_000_000, transcendentals=TOKENS * FF),
+        cost_estimate=pl.CostEstimate(flops=6 * TOKENS * D * FF, bytes_accessed=200_000_000, transcendentals=TOKENS * FF),
         name=f"gather_{number}",
-    )(a, wgu, wd)
+    )(a, wgu, wd, other)
     return g_gu.reshape(2, D, FF), g_d.reshape(FF, D), *rest
 
 
 DC = 128
 NDC = D // DC
-TAIL = 7
 
 
 class Summing:
     HEIGHTS = {"gu": ((RD, RD), (RD, RD)), "d": ((40, 40), (40, RF - 120))}
 
-    def __init__(self, kind, count, entry, me, own, inbox, s1, r2, s2, r3, acc, s4, r4, s5, r5, xb, ssem, rsem, out):
-        self.kind, self.count, self.entry, self.me = kind, count, entry, me
+    def __init__(self, kind, count, stride, lag, me, own, inbox, s1, r2, s2, r3, acc, s4, r4, s5, r5, xb, ssem, rsem, out):
+        self.kind, self.count, self.stride, self.lag, self.me = kind, count, stride, lag, me
+        self.big, self.small, self.sent = slots(stride, lag)
         self.own, self.inbox, self.s1, self.r2, self.s2, self.r3 = own, inbox, s1, r2, s2, r3
         self.acc, self.s4, self.r4, self.s5, self.r5, self.xb = acc, s4, r4, s5, r5, xb
         self.ssem, self.rsem, self.out = ssem, rsem, out
         self.subs = (slice(None),) if kind == "gu" else (0, 1)
+
+    def due(self, i, k):
+        passed = i - 1 - k * self.lag
+        t = lax.div(passed, self.stride)
+        return t, (passed >= 0) & (t < self.count) & (lax.rem(passed, self.stride) == 0)
 
     def part(self, half, sub):
         if self.kind == "gu":
@@ -260,7 +286,7 @@
         return self.inbox.at[(slot, *((0,), (pl.ds(0, 2),), (0, 0), (0, pl.ds(0, 2)))[k - 1])]
 
     def compute(self, k, t):
-        me, slot, two = self.me, lax.rem(t, 4), lax.rem(t, 2)
+        me, slot, two, sent = self.me, lax.rem(t, self.big), lax.rem(t, self.small), lax.rem(t, self.sent)
         if k > 0:
             wait_bytes(self.size(k - 1, slot, two), self.rsem.at[k - 1, slot])
             wait_bytes(self.size(k - 1, slot, two), self.ssem.at[k - 1, slot])
@@ -279,25 +305,25 @@
             for sub in (0, 1):
                 rows = self.rows(half, sub)
                 if k == 1:
-                    self.s1[half, sub, :, rows] = self.both(slot, *along(me.ring(first, 2)), half, sub).astype(BF)
+                    self.s1[sent, half, sub, :, rows] = self.both(slot, *along(me.ring(first, 2)), half, sub).astype(BF)
                 if k == 2:
                     for way, by in ((0, 1), (1, 3)):
                         term = self.both(slot, *along(me.ring(first, by)), half, sub)
                         if sub == way:
                             term = term + self.r2[two, half, sub, :, rows].astype(F32)
-                        self.s2[half, way, sub, :, rows] = term.astype(BF)
+                        self.s2[sent, half, way, sub, :, rows] = term.astype(BF)
                 if k == 3:
                     term = self.both(slot, *along(me.pos[first]), half, sub)
                     for way in (0, 1):
                         term = term + self.r3[two, half, way, sub, :, rows].astype(F32)
                     self.acc[two, half, sub, :, rows] = term
-                    self.s4[half, sub, rows] = self.acc[two, half, sub, me.ring(second, 2), rows].astype(BF)
+                    self.s4[sent, half, sub, rows] = self.acc[two, half, sub, me.ring(second, 2), rows].astype(BF)
                 if k == 4:
                     for way, by in ((0, 1), (1, 3)):
                         term = self.acc[two, half, sub, me.ring(second, by), rows]
                         if sub == way:
                             term = term + self.r4[two, half, sub, rows].astype(F32)
-                        self.s5[half, way, sub, rows] = term.astype(BF)
+                        self.s5[sent, half, way, sub, rows] = term.astype(BF)
                 if k == 5:
                     term = self.acc[two, half, sub, me.pos[second], rows]
                     for way in (0, 1):
@@ -309,7 +335,7 @@
                         self.xb[two, me.x, where, columns] = term.astype(BF)
 
     def send(self, k, t, source=None):
-        me, slot, two = self.me, lax.rem(t, 4), lax.rem(t, 2)
+        me, slot, two, sent = self.me, lax.rem(t, self.big), lax.rem(t, self.small), lax.rem(t, self.sent)
 
         def go(src, dst, peer):
             pltpu.make_async_remote_copy(
@@ -326,41 +352,50 @@
             for way, by in ((0, 1), (1, 3)):
                 if k == 1:
                     rows = self.rows(half, way)
-                    go(self.s1.at[half, way, :, rows], self.r2.at[two, half, way, :, rows], me.near(first, by))
+                    go(self.s1.at[sent, half, way, :, rows], self.r2.at[two, half, way, :, rows], me.near(first, by))
                 if k == 3:
                     rows = self.rows(half, way)
-                    go(self.s4.at[half, way, rows], self.r4.at[two, half, way, rows], me.near(second, by))
+                    go(self.s4.at[sent, half, way, rows], self.r4.at[two, half, way, rows], me.near(second, by))
                 if k in (2, 4):
                     for sub in self.subs:
                         rows = self.rows(half, sub)
                         if k == 2:
-                            go(self.s2.at[half, way, sub, :, rows], self.r3.at[two, half, way, sub, :, rows], me.near(first, by))
+                            go(self.s2.at[sent, half, way, sub, :, rows], self.r3.at[two, half, way, sub, :, rows], me.near(first, by))
                         else:
-                            go(self.s5.at[half, way, sub, rows], self.r5.at[two, half, way, sub, rows], me.near(second, by))
-
-
-def stage_buffers(kind):
+                            go(self.s5.at[sent, half, way, sub, rows], self.r5.at[two, half, way, sub, rows], me.near(second, by))
+
+
+def slots(stride, lag):
+    return -(-4 * lag // stride), -(-2 * lag // stride), -(-lag // stride)
+
+
+def stage_buffers(kind, stride, lag):
     block = (2, NY, NZ, RD, TF) if kind == "gu" else (NY, NZ, RF, DC)
     last = (2, RD, TF) if kind == "gu" else (RF, DC)
+    big, small, sent = slots(stride, lag)
     return [
-        pltpu.VMEM((4, 2, NY, NZ, 2, RD, TF) if kind == "gu" else (4, *block), BF),
-        pltpu.VMEM((4, *block), BF),
-        pltpu.VMEM((2, 2, 4, 40, 128), BF),
-        pltpu.VMEM((2, 2, 2, 4, 40, 128), BF),
-        pltpu.VMEM((2, 2, 2, 4, 40, 128), BF),
-        pltpu.VMEM((2, 2, 2, 2, 4, 40, 128), BF),
-        pltpu.VMEM((2, 2, 2, 4, 40, 128), F32),
-        pltpu.VMEM((2, 2, 40, 128), BF),
-        pltpu.VMEM((2, 2, 2, 40, 128), BF),
-        pltpu.VMEM((2, 2, 2, 40, 128), BF),
-        pltpu.VMEM((2, 2, 2, 2, 40, 128), BF),
-        pltpu.VMEM((2, NX, *last), BF),
-        pltpu.SemaphoreType.DMA((6, 4)),
-        pltpu.SemaphoreType.DMA((6, 4)),
+        pltpu.VMEM((big, 2, NY, NZ, 2, RD, TF) if kind == "gu" else (big, *block), BF),
+        pltpu.VMEM((big, *block), BF),
+        pltpu.VMEM((sent, 2, 2, 4, 40, 128), BF),
+        pltpu.VMEM((small, 2, 2, 4, 40, 128), BF),
+        pltpu.VMEM((sent, 2, 2, 2, 4, 40, 128), BF),
+        pltpu.VMEM((small, 2, 2, 2, 4, 40, 128), BF),
+        pltpu.VMEM((small, 2, 2, 4, 40, 128), F32),
+        pltpu.VMEM((sent, 2, 2, 40, 128), BF),
+        pltpu.VMEM((small, 2, 2, 40, 128), BF),
+        pltpu.VMEM((sent, 2, 2, 2, 40, 128), BF),
+        pltpu.VMEM((small, 2, 2, 2, 40, 128), BF),
+        pltpu.VMEM((small, NX, *last), BF),
+        pltpu.SemaphoreType.DMA((6, big)),
+        pltpu.SemaphoreType.DMA((6, big)),
     ]
 
 
 NBUF = 14
+
+
+def pace(with_da):
+    return (1, 1) if with_da else (2, 2)
 
 
 def back_kernel(with_da, *refs):
@@ -371,7 +406,7 @@
     out_gu, out_d = take(2)
     da = take(1)[0] if with_da else None
     gu_bufs, d_bufs = take(NBUF), take(NBUF)
-    dg_s, du_s, lsem = take(3)
+    dgu_s, lsem = take(2)
     i = pl.program_id(0)
     me = Place()
 
@@ -380,17 +415,19 @@
         me.meet(True)
 
     own = gu_bufs[0]
-    gu = Summing("gu", NT, 1, me, *gu_bufs, out_gu)
-    down = Summing("d", NDC, 1, me, *d_bufs, out_d)
+    lag, stride = pace(with_da)
+    gu = Summing("gu", NT, 1, lag, me, *gu_bufs, out_gu)
+    down = Summing("d", NDC, stride, lag, me, *d_bufs, out_d)
 
     def load(n):
-        return pltpu.make_async_copy(dwd.at[:, :, me.c, :, cols(n * DC, DC)], down.own.at[lax.rem(n, 4)], lsem.at[lax.rem(n, 4)])
+        slot = lax.rem(n, down.big)
+        return pltpu.make_async_copy(dwd.at[:, :, me.c, :, cols(n * DC, DC)], down.own.at[slot], lsem.at[slot])
 
     for k in (6, 5, 4, 3, 2, 1):
         for engine in (gu, down):
-            t = i - engine.entry - k
-
-            @pl.when((t >= 0) & (t < engine.count))
+            t, there = engine.due(i, k)
+
+            @pl.when(there)
             def _(k=k, engine=engine, t=t):
                 if k == 1 and engine is down:
                     load(t).wait()
@@ -398,48 +435,44 @@
 
     for k in (5, 4, 3, 2, 1, 0):
         for engine in (gu, down):
-            t = i - engine.entry - k
-
-            @pl.when((t >= 0) & (t < engine.count))
+            t, there = engine.due(i, k)
+
+            @pl.when(there)
             def _(k=k, engine=engine, t=t):
                 source = None
                 if k == 0:
-                    source = own.at[lax.rem(t, 4), :, :, :, 1 - me.c] if engine is gu else dwd.at[:, :, 1 - me.c, :, cols(t * DC, DC)]
+                    source = own.at[lax.rem(t, gu.big), :, :, :, 1 - me.c] if engine is gu else dwd.at[:, :, 1 - me.c, :, cols(t * DC, DC)]
                 engine.send(k, t, source)
 
-    @pl.when(i < NDC)
-    def _():
-        load(i).start()
+    @pl.when((i < NDC * stride) & (lax.rem(i, stride) == 0))
+    def _():
+        load(lax.div(i, stride)).start()
 
     @pl.when(i < NT)
     def _():
-        slot = lax.rem(i, 4)
-        rows = TOKENS // 4
-        for r in range(4):
-            part = pl.ds(r * rows, rows)
-            dh = dot(dy[part, :], wd[...], 1, 1).astype(BF).astype(F32)
-            g, u = gate[part, :], up[part, :]
-            sg = jax.nn.sigmoid(g)
-            du_s[part, :] = (dh * (g * sg)).astype(BF)
-            dg_s[part, :] = (dh * u * (sg * (1 + g * (1 - sg)))).astype(BF)
-        own[slot, 0] = dot(a[...], dg_s[...], 0, 0).reshape(NY, NZ, 2, RD, TF).astype(BF)
-        own[slot, 1] = dot(a[...], du_s[...], 0, 0).reshape(NY, NZ, 2, RD, TF).astype(BF)
+        slot = lax.rem(i, gu.big)
+        dh = dot(dy[...], wd[...], 1, 1).astype(BF).astype(F32)
+        g, u = gate[...], up[...]
+        sg = jax.nn.sigmoid(g)
+        dgu_s[:, TF:] = (dh * (g * sg)).astype(BF)
+        dgu_s[:, :TF] = (dh * u * (sg * (1 + g * (1 - sg)))).astype(BF)
+        own[slot, 0] = dot(a[...], dgu_s[:, :TF], 0, 0).reshape(NY, NZ, 2, RD, TF).astype(BF)
+        own[slot, 1] = dot(a[...], dgu_s[:, TF:], 0, 0).reshape(NY, NZ, 2, RD, TF).astype(BF)
         if with_da:
-            for r in range(4):
-                part = pl.ds(r * rows, rows)
-                more = dot(dg_s[part, :], wgu[0], 1, 1) + dot(du_s[part, :], wgu[1], 1, 1)
-
-                @pl.when(i == 0)
-                def _():
-                    da[part, :] = more
-
-                @pl.when(i > 0)
-                def _():
-                    da[part, :] += more
+            more = dot(dgu_s[...], jnp.concatenate([wgu[0], wgu[1]], 1), 1, 1)
+
+            @pl.when(i == 0)
+            def _():
+                da[...] = more
+
+            @pl.when(i > 0)
+            def _():
+                da[...] += more
 
 
 def backward(a, dy, g_d, gate, up, dwd, g_gu, number):
     with_da = g_gu is not None
+    lag, stride = pace(with_da)
     last = lambda i: upto(i, NT - 1)
     vmem, hbm = pl.BlockSpec(memory_space=pltpu.VMEM), pl.BlockSpec(memory_space=pl.ANY)
     tile = pl.BlockSpec((TOKENS, TF), lambda i: (0, last(i)))
@@ -452,16 +485,15 @@
         operands.append(g_gu)
     return pl.pallas_call(
         functools.partial(back_kernel, with_da),
-        grid=(NT + TAIL,),
+        grid=(NT + 1 + 6 * lag,),
         in_specs=in_specs,
         out_specs=[vmem] * len(out_shape),
         out_shape=out_shape,
         scratch_shapes=[
-            *stage_buffers("gu"),
-            *stage_buffers("d"),
-            pltpu.VMEM((TOKENS, TF), BF),
-            pltpu.VMEM((TOKENS, TF), BF),
-            pltpu.SemaphoreType.DMA((4,)),
+            *stage_buffers("gu", 1, lag),
+            *stage_buffers("d", stride, lag),
+            pltpu.VMEM((TOKENS, 2 * TF), BF),
+            pltpu.SemaphoreType.DMA((slots(stride, lag)[0],)),
         ],
         compiler_params=pltpu.CompilerParams(
             collective_id=number, has_side_effects=True, vmem_limit_bytes=VMEM_LIMIT, dimension_semantics=("arbitrary",)
@@ -541,11 +573,9 @@
         shards = lambda layer: (jnp.stack([weights[0][layer], weights[1][layer]]), weights[2][layer])
         h0, dy = x[0], dy[0]
         a0 = normed(h0)
-        gu0, d0, act0, gate0, up0 = gathered(a0, *shards(0), 0)
-        h1 = h0 + dot(act0, d0, 1, 0).astype(BF)
+        _, d0, act0, gate0, up0, h1 = gathered(a0, *shards(0), h0, 0)
         a1, back = jax.vjp(normed, h1)
-        gu1, d1, act1, gate1, up1 = gathered(a1, *shards(1), 1)
-        by_d1 = dot(act1, dy, 0, 0).astype(BF)
+        gu1, d1, gate1, up1, by_d1 = gathered(a1, *shards(1), dy, 1)
         mine_gu1, mine_d1, da = backward(a1, dy, d1, gate1, up1, by_d1, gu1, 2)
         dh = dy + back(da.astype(BF))[0]
         by_d0 = dot(act0, dh, 0, 0).astype(BF)

time: 806 us -> 867 us (1.076)
  Pallas kernels: 647 us -> 779 us
  matrix products: 102 us -> 34.5 us
    pallas_call x4, Pallas kernels: 629 us -> 763 us  [the longest x2 470 us: backward(): pl.pallas_call(functools.partial(back_kernel, with_da), grid=(NT + 1 + 6...]
    dot_general x3 -> x1, matrix products: 102 us -> 34.5 us  [dot(): lax.dot_general(a, b, (((ca,), (cb,)), ((), ())), preferred_element_type=...]
where the time goes in v2:
time: 867 us; the launch traced here: 870 us
  Pallas kernels  779 us (90%)
  other arithmetic  40.9 us (5%)
  matrix products  34.5 us (4%)
  local copies, waits for them, and re-layouts  11.4 us (1%)
    pallas_call x2, Pallas kernels, backward(): pl.pallas_call(functools.partial(back_kernel, with_da), grid=(NT + 1 + 6...  470 us
    pallas_call x2, Pallas kernels, gathered(): pl.pallas_call(functools.partial(gather_kernel, forward), grid=(LEAD + CH...  293 us
    dot_general x1, matrix products, dot(): lax.dot_general(a, b, (((ca,), (cb,)), ((), ())), preferred_element_type=...  34.5 us

profile of v2, /device:TPU:1, one launch (start us, length us, event | category | flops | bytes accessed | tf_op | source)
XLA Modules:
  0.0 869.7 jit_solution(11660642816357916046)
XLA Ops:
  0.7 3.7 fusion
  4.5 1.0 copy-done.10
  5.6 1.3 pad_maximum_fusion
  7.8 3.2 fusion.1.refs_0_
  11.0 141.6 %gather_0.1 = (bf16[2,4,4,2,40,4864]{5,4,3,2,1,0:T(8,128)(2,1)}, bf16[4,4,2,152,1280]{4,3,2,1,0:T(8,128)(2,1)}, bf16[2048,4864]{1,0:T(8,128)(2,1)}, f32[2048,486...) custom-call(bf16[2048,1280]{1,0:T(8,128)(2,1)} %fusion.1.refs_0_, ...), custom_call_target="tpu_custom_call" | custom-call | flops 76504104960 | bytes 200000000 | tf_op jit(solution)/shard_map/gather_0/pallas_call | solution.py:217
  152.7 3.7 fusion.4
  157.6 3.2 fusion.5.refs_0_
  160.8 151.8 %gather_1.1 = (bf16[2,4,4,2,40,4864]{5,4,3,2,1,0:T(8,128)(2,1)}, bf16[4,4,2,152,1280]{4,3,2,1,0:T(8,128)(2,1)}, f32[2048,4864]{1,0:T(8,128)}, f32[2048,4864]{1,0:T(8,128)}, bf16[4864,1280]{1,0:T(8,128)(2,1)}) custom-call(bf16[2048,1280]{1,0:T(8,128)(2,1)} %fusion.5.refs_0_, bf16[2,40,4864]{2,1,0:T(8,128)(2,1)} %get-tuple-element.59.refs_1_, ...), custom_call_target="tpu_custom_call" | custom-call | flops 76504104960 | bytes 200000000 | tf_op jit(solution)/shard_map/gather_1/pallas_call | solution.py:217
  312.6 261.8 %backward_2.1 = (bf16[2,40,4864]{2,1,0:T(8,128)(2,1)}, bf16[152,1280]{1,0:T(8,128)(2,1)}, f32[2048,1280]{1,0:T(8,128)}) custom-call(bf16[2048,1280]{1,0:T(8,128)(2,1)} %fusion.5.refs_0_, bf16[2048,1280]{1,0:T(8,128)(2,1)} %bitcast.23, bf16[4864,1280]{1,0:T(8,128)(2,1)} %bitcast.30, f32[2048,4864]{1,0:T(8,128)} %get-tuple-element.26.refs_3_, ...), custom_call_target="tpu_custom_call" | custom-call | flops 127506841600 | bytes 200000000 | tf_op jit(solution)/shard_map/backward_2/pallas_call | solution.py:486
  574.5 2.0 fusion.37
  576.5 6.8 fusion.6
  583.5 1.6 copy-done.2
  585.1 5.8 fusion.7.refs_1_
  590.9 34.5 %convolution_convert_fusion = bf16[4864,1280]{1,0:T(8,128)(2,1)} fusion(bf16[2048,4864]{1,0:T(8,128)(2,1)} %get-tuple-element.34, bf16[2048,1280]{1,0:T(8,128)(2,1)S(1)} %fusion.7.refs_1_), kind=kOutput, calls=%fused_computation | convolution fusion | flops 25507594240 | bytes 37617664 | tf_op jit(solution)/shard_map/dot_general | solution.py:25
  625.4 207.9 %backward_3.1 = (bf16[2,40,4864]{2,1,0:T(8,128)(2,1)}, bf16[152,1280]{1,0:T(8,128)(2,1)}) custom-call(bf16[2048,1280]{1,0:T(8,128)(2,1)} %fusion.1.refs_0_, bf16[2048,1280]{1,0:T(8,128)(2,1)} %copy-done.3, bf16[4864,1280]{1,0:T(8,128)(2,1)} %bitcast.29, f32[2048,4864]{1,0:T(8,128)} %get-tuple-element.32.refs_3_, f32[2048,4864]{1,0:T(8,128)} %get-tuple-element.33.refs_4_, ...), custom_call_target="tpu_custom_call" | custom-call | flops 76504104960 | bytes 200000000 | tf_op jit(solution)/shard_map/backward_3/pallas_call | solution.py:486
  833.3 2.2 fusion.19
  835.5 1.3 fusion.36
  836.8 1.0 fusion.17
  841.4 16.0 %total.1 = f32[8,128]{1,0:T(8,128)} custom-call(f32[8,128]{1,0:T(8,128)} %broadcast_in_dim.2.part), custom_call_target="tpu_custom_call" | custom-call | tf_op jit(solution)/shard_map/total/pallas_call | solution.py:534
  857.4 1.2 slice.43
  859.4 4.3 fusion.25
  863.7 2.3 fusion.16
  866.1 1.1 copy-done.17
  867.2 2.3 fusion.22
  (54 shorter events, 4.2 us)
Async XLA Ops:
  0.6 3.8 copy-start.8
  0.7 7.2 slice-start
  4.4 1.1 copy-start.10
  4.4 3.4 slice-start.1
  5.6 1.3 copy-start.6
  152.7 4.9 copy-start
  156.4 0.6 copy-start.18
  157.0 0.6 copy-start.20
  576.5 6.8 copy-start.19
  576.5 7.0 copy-start.1
  576.5 8.6 copy-start.2
  576.5 8.6 copy-start.21
  590.9 34.5 %copy-start.3 = (bf16[2048,1280]{1,0:T(8,128)(2,1)}, bf16[2048,1280]{1,0:T(8,128)(2,1)S(1)}, u32[]{:S(2)}) copy-start(bf16[2048,1280]{1,0:T(8,128)(2,1)S(1)} %fusion.7.refs_1_) | copy-start | bytes 15728644
  833.3 3.5 copy-start.5
  833.3 4.5 copy-start.4
  835.5 23.8 %copy-start.7 = (bf16[2,152,1280]{2,1,0:T(8,128)(2,1)S(1)}, bf16[2,152,1280]{2,1,0:T(8,128)(2,1)}, u32[]{:S(2)}) copy-start(bf16[2,152,1280]{2,1,0:T(8,128)(2,1)} %param.15) | copy-start | bytes 2334724
  835.5 23.8 %copy-start.12 = (bf16[152,1280]{1,0:T(8,128)(2,1)S(1)}, bf16[152,1280]{1,0:T(8,128)(2,1)}, u32[]{:S(2)}) copy-start(bf16[152,1280]{1,0:T(8,128)(2,1)} %get-tuple-element.38) | copy-start | bytes 1167364
  835.5 23.8 %copy-start.13 = (bf16[152,1280]{1,0:T(8,128)(2,1)S(1)}, bf16[152,1280]{1,0:T(8,128)(2,1)}, u32[]{:S(2)}) copy-start(bf16[152,1280]{1,0:T(8,128)(2,1)} %get-tuple-element.37) | copy-start | bytes 1167364
  859.3 4.4 copy-start.9
  859.3 4.4 copy-start.14
  859.3 4.4 copy-start.15
  863.7 2.4 copy-start.11
  863.7 2.4 copy-start.16
  863.7 3.5 copy-start.17

commit v3 on v2

v3 whole, which is shorter than its diff:
```python
import functools

import jax
import jax.numpy as jnp
from jax import lax
from jax.experimental import pallas as pl
from jax.experimental.pallas import tpu as pltpu
from jax.sharding import PartitionSpec as P

NAMES = ("w_gate", "w_up", "w_down")
BF, F32 = jnp.bfloat16, jnp.float32
MESH = pl.DeviceIdType.MESH

TOKENS, D, FF = 2048, 1280, 4864
NY = NZ = NX = 4
S = NY * NZ * 2
RD, RF = D // S, FF // S
TF = 256
NT = FF // TF
ND = D // TF
VMEM_LIMIT = 67_000_000
AXES = ((0, 1), (1, 0))
WAYS = ((0, 1), (1, 3))


def dot(a, b, ca, cb):
    return lax.dot_general(a, b, (((ca,), (cb,)), ((), ())), preferred_element_type=F32)


def at(*index):
    return index


def above(i):
    return i * ((i + 64) // 64)


def upto(i, last):
    return last - above(last - i)


def cols(start, size):
    return pl.ds(pl.multiple_of(start, 128), size)


class Place:
    def __init__(self):
        s = lax.axis_index("s")
        self.y, self.z, self.c = lax.div(s, NZ * 2), lax.rem(lax.div(s, 2), NZ), lax.rem(s, 2)
        self.x = lax.axis_index("r")
        self.pos = (self.y, self.z)

    def ring(self, axis, by):
        return lax.rem(self.pos[axis] + by, 4)

    def near(self, axis, by):
        y, z = (self.ring(0, by), self.z) if axis == 0 else (self.y, self.ring(1, by))
        return {"s": (y * NZ + z) * 2 + self.c}

    def partner(self):
        return {"s": (self.y * NZ + self.z) * 2 + 1 - self.c}

    def across(self, by):
        return {"r": lax.rem(self.x + by, NX)}

    def meet(self, x_too):
        barrier = pltpu.get_barrier_semaphore()
        peers = [self.near(axis, by) for axis in (0, 1) for by in (1, 3)] + [self.partner()]
        if x_too:
            peers += [self.across(by) for by in (1, 2, 3)]
        for peer in peers:
            pl.semaphore_signal(barrier, inc=1, device_id=peer, device_id_type=MESH)
        pl.semaphore_wait(barrier, len(peers))


def wait_bytes(ref, sem):
    pltpu.make_async_copy(ref, ref, sem).wait()


CH = NT + 2
LAG = 2
LEAD = 5 * LAG + 1
STAGES = 7
ALONG_X = (-7, -5, -3, -1, 1, 9, 13, NT - 1)
WITHIN = (3, 5, 7, 9, None, None, 11, NT - 1)


def gather_kernel(forward, *refs):
    if forward:
        h, wgu, wd, g_gu, g_d, a_out, act, gate, up, h_new, wt, wdt, act_s, a, ssem, rsem, lsem, osem = refs
    else:
        h, wgu, wd, dy, g_gu, g_d, a_out, gate, up, dwd, wt, act_s, a, ssem, rsem, lsem, osem = refs
    step = pl.program_id(0)
    i = step - LEAD
    me = Place()
    own = [
        pltpu.make_async_copy(wgu, g_gu.at[:, me.y, me.z, me.c], osem.at[0]),
        *(
            pltpu.make_async_copy(wd.at[:, cols(t * TF, TF)], g_d.at[me.y, me.z, me.c, :, cols(t * TF, TF)], osem.at[n])
            for n, t in ((1, me.x), (2, ND - 1))
        ),
    ]

    @pl.when(step == 0)
    def _():
        me.meet(True)
        for copy in own:
            copy.start()

    @pl.when(step == 2 * LAG)
    def _():
        for copy in own:
            copy.wait()

    def block(kind, t, half, sub, y, z, c):
        width = TF if half is None else TF // 2
        start = t * TF + (half or 0) * (TF // 2)
        if kind == "gu":
            lead = slice(None) if sub is None else sub
            return g_gu.at[lead, y, z, c, :, cols(start, width)]
        rows = {None: slice(None), 0: pl.ds(0, 80), 1: pl.ds(80, RF - 80)}[sub]
        return g_d.at[y, z, c, rows, cols(start, width)]

    def mine(kind, t, half):
        start = t * TF + half * (TF // 2)
        return wgu.at[:, :, cols(start, TF // 2)] if kind == "gu" else wd.at[:, cols(start, TF // 2)]

    ALL = slice(None)

    def cores(kind, t, c):
        return g_d.at[:, :, c, :, 0 : NX * TF] if kind == "x" else block(kind, t, None, None, ALL, ALL, c)

    def totals(kind, t, k):
        c = me.c
        if k == 6:
            return cores(kind, t, c)
        y, z, c = [(pl.ds(0, 2), 0, c), (pl.ds(0, 1), 0, c), (ALL, pl.ds(0, 2), c), (ALL, pl.ds(0, 1), c), (ALL, ALL, ALL), (ALL, ALL, c)][k]
        return block(kind, t, None, None, y, z, c)

    def send(kind, t, ch, k):
        def go(src, dst, peer):
            pltpu.make_async_remote_copy(
                src_ref=src, dst_ref=dst, send_sem=ssem.at[k, ch], recv_sem=rsem.at[k, ch], device_id=peer, device_id_type=MESH
            ).start()

        y, z, c = me.y, me.z, me.c
        if k < 4:
            for half in (0, 1):
                first, second = AXES[half]
                if k == 0:
                    for by in (1, 3):
                        go(mine(kind, t, half), block(kind, t, half, None, y, z, c), me.near(first, by))
                if k == 1:
                    for sub, by in WAYS:
                        back = me.ring(first, 4 - by)
                        ref = block(kind, t, half, sub, *((back, z) if first == 0 else (y, back)), c)
                        go(ref, ref, me.near(first, by))
                if k == 2:
                    ref = block(kind, t, half, None, *((ALL, z) if first == 0 else (y, ALL)), c)
                    for by in (1, 3):
                        go(ref, ref, me.near(second, by))
                if k == 3:
                    for sub, by in WAYS:
                        back = me.ring(second, 4 - by)
                        ref = block(kind, t, half, sub, *((ALL, back) if second == 1 else (back, ALL)), c)
                        go(ref, ref, me.near(second, by))
        if k == 4:
            ref = block(kind, t, None, None, ALL, ALL, c)
            for by in (1, 3):
                go(ref, ref, me.across(by))
        if k == 5:
            for sub, by in WAYS:
                ref = block(kind, lax.rem(me.x + 4 - by, NX), None, sub, ALL, ALL, c)
                go(ref, ref, me.across(by))
        if k == 6:
            ref = cores(kind, t, c)
            go(ref, ref, me.partner())

    def load(kind, t):
        slot = lax.rem(t, 2)
        if kind == "gu":
            return pltpu.make_async_copy(g_gu.at[:, :, :, :, :, cols(t * TF, TF)], wt.at[slot], lsem.at[0, slot])
        return pltpu.make_async_copy(g_d.at[:, :, :, :, cols(t * TF, TF)], wdt.at[slot], lsem.at[1, slot])

    PLANE = (0, 1, 2, 3, 6)

    save = pltpu.make_async_copy(a, a_out, osem.at[3])

    @pl.when(step == 1)
    def _():
        rows = TOKENS // 4
        for r in range(4):
            part = pl.ds(r * rows, rows)
            a[part, :] = normed(h[part, :])

    @pl.when(step == 2)
    def _():
        save.start()

    for n in (5, 4, 3, 2, 1, 0):
        t = i + 1 + (5 - n) * LAG

        @pl.when((t >= 0) & (t < NT))
        def _(n=n, t=t):
            if n > 0:
                wait_bytes(totals("gu", t, PLANE[n - 1]), rsem.at[PLANE[n - 1], t])
            if n < 5:
                send("gu", t, t, PLANE[n])
            else:
                load("gu", t).start()

    for kind, t, ch, due in (("x", me.x, NT, ALONG_X), ("d", ND - 1, NT + 1, WITHIN)):
        stages = [k for k in range(STAGES + 1) if due[k] is not None]
        for before, k in zip([None, *stages], stages):

            @pl.when(i == due[k])
            def _(kind=kind, t=t, ch=ch, before=before, k=k):
                if before is not None:
                    wait_bytes(totals(kind, t, before), rsem.at[before, ch])
                if k < STAGES:
                    send(kind, t, ch, k)

    if forward:

        @pl.when((i >= NT - 1) & (i < NT + ND - 1))
        def _():
            load("d", i - NT + 1).start()

    @pl.when((i >= 0) & (i < NT))
    def _():
        load("gu", i).wait()
        slot = lax.rem(i, 2)
        g = dot(a[...], wt[slot, 0].reshape(D, TF), 1, 0)
        u = dot(a[...], wt[slot, 1].reshape(D, TF), 1, 0)
        gate[...] = g
        up[...] = u
        hidden = (g * jax.nn.sigmoid(g) * u).astype(BF)
        if forward:
            act[...] = hidden
            act_s[:, cols(i * TF, TF)] = hidden
        else:
            act_s[...] = hidden
            dwd[...] = dot(act_s[...], dy[...], 0, 0).astype(BF)

    if forward:

        @pl.when(i >= NT)
        def _():
            load("d", i - NT).wait()
            h_new[...] = h[:, cols((i - NT) * TF, TF)] + dot(act_s[...], wdt[lax.rem(i - NT, 2)].reshape(FF, TF), 1, 0).astype(BF)

    @pl.when(step == pl.num_programs(0) - 1)
    def _():
        save.wait()
        for k in PLANE:

            @pl.loop(0, NT)
            def _(t, k=k):
                wait_bytes(totals("gu", t, k), ssem.at[k, t])

        for kind, t, ch, due in (("x", me.x, NT, ALONG_X), ("d", ND - 1, NT + 1, WITHIN)):
            for k in range(STAGES):
                if due[k] is not None:
                    wait_bytes(totals(kind, t, k), ssem.at[k, ch])


def gathered(h, wgu, wd, dy, number):
    forward = dy is None
    vmem, hbm = pl.BlockSpec(memory_space=pltpu.VMEM), pl.BlockSpec(memory_space=pl.ANY)
    tile = pl.BlockSpec((TOKENS, TF), lambda step: (0, upto(above(step - LEAD), NT - 1)))
    column = pl.BlockSpec((TOKENS, TF), lambda step: (0, above(step - LEAD - NT)))
    row = pl.BlockSpec((TF, D), lambda step: (upto(above(step - LEAD), NT - 1), 0))
    shape, sems = jax.ShapeDtypeStruct, pltpu.SemaphoreType.DMA
    wide = [shape((TOKENS, FF), F32)] * 2
    states = shape((TOKENS, D), BF)
    g_gu, g_d, *rest = pl.pallas_call(
        functools.partial(gather_kernel, forward),
        grid=(LEAD + NT + (ND if forward else 0),),
        in_specs=[vmem, vmem, vmem] + ([] if forward else [vmem]),
        out_specs=[hbm, hbm, hbm, *([tile] * 3 + [column] if forward else [tile, tile, row])],
        out_shape=[
            shape((2, NY, NZ, 2, RD, FF), BF),
            shape((NY, NZ, 2, RF, D), BF),
            states,
            *([shape((TOKENS, FF), BF), *wide, states] if forward else [*wide, shape((FF, D), BF)]),
        ],
        scratch_shapes=[
            pltpu.VMEM((2, 2, NY, NZ, 2, RD, TF), BF),
            *([pltpu.VMEM((2, NY, NZ, 2, RF, TF), BF), pltpu.VMEM((TOKENS, FF), BF)] if forward else [pltpu.VMEM((TOKENS, TF), BF)]),
            pltpu.VMEM((TOKENS, D), BF),
            sems((STAGES, CH)),
            sems((STAGES, CH)),
            sems((2, 2)),
            sems((4,)),
        ],
        compiler_params=pltpu.CompilerParams(
            collective_id=number, has_side_effects=True, vmem_limit_bytes=VMEM_LIMIT, dimension_semantics=("arbitrary",)
        ),
        cost_estimate=pl.CostEstimate(flops=6 * TOKENS * D * FF, bytes_accessed=200_000_000, transcendentals=TOKENS * FF),
        name=f"gather_{number}",
    )(h, wgu, wd, *([] if forward else [dy]))
    return g_gu.reshape(2, D, FF), g_d.reshape(FF, D), *rest


DC = 128
STRIDE = {"gu": 1, "d": 2}
BIG, SMALL = {"gu": 4, "d": 2}, 2
NR = 8
NDC = D // DC


class Summing:
    HEIGHTS = {"gu": ((RD, RD), (RD, RD)), "d": ((40, 40), (40, RF - 120))}

    def __init__(self, kind, count, me, own, inbox, s1, r2, s2, r3, acc, s4, r4, s5, r5, xb, ssem, rsem, out):
        self.kind, self.count, self.me = kind, count, me
        self.stride, self.big = STRIDE[kind], BIG[kind]
        self.own, self.inbox, self.s1, self.r2, self.s2, self.r3 = own, inbox, s1, r2, s2, r3
        self.acc, self.s4, self.r4, self.s5, self.r5, self.xb = acc, s4, r4, s5, r5, xb
        self.ssem, self.rsem, self.out = ssem, rsem, out
        self.subs = (slice(None),) if kind == "gu" else (0, 1)

    def due(self, i, k):
        passed = i - 1 - k
        t = lax.div(passed, self.stride)
        return t, (passed >= 0) & (t < self.count) & (lax.rem(passed, self.stride) == 0)

    def part(self, half, sub):
        if self.kind == "gu":
            return sub, slice(None), pl.ds(half * 128, 128)
        low = 80 * half + 40 * sub
        return 0, pl.ds(low, self.HEIGHTS["d"][half][sub]), slice(None)

    def rows(self, half, sub):
        return slice(None) if self.kind == "gu" else pl.ds(0, self.HEIGHTS["d"][half][sub])

    def both(self, slot, y, z, half, sub):
        lead, rows, columns = self.part(half, sub)
        mine = self.own[slot, lead, y, z, self.me.c, rows, columns] if self.kind == "gu" else self.own[slot, y, z, rows, columns]
        theirs = self.inbox[slot, lead, y, z, rows, columns] if self.kind == "gu" else self.inbox[slot, y, z, rows, columns]
        return mine.astype(F32) + theirs.astype(F32)

    def size(self, k, slot, two):
        if k == 0:
            return self.inbox.at[slot]
        if k == 5:
            return self.xb.at[two, pl.ds(0, 3)]
        if self.kind == "gu":
            return (self.r2, self.r3, self.r4, self.r5)[k - 1].at[two]
        return self.inbox.at[(slot, *((0,), (pl.ds(0, 2),), (0, 0), (0, pl.ds(0, 2)))[k - 1])]

    def compute(self, k, t):
        me, slot, two = self.me, lax.rem(t, self.big), lax.rem(t, SMALL)
        if k > 0:
            wait_bytes(self.size(k - 1, slot, two), self.rsem.at[k - 1, slot])
            wait_bytes(self.size(k - 1, slot, two), self.ssem.at[k - 1, slot])
        if k == 6:
            total = self.xb[two, 0].astype(F32)
            for x in range(1, NX):
                total = total + self.xb[two, x].astype(F32)
            if self.kind == "gu":
                self.out[:, :, cols(t * TF, TF)] = total.astype(BF)
            else:
                self.out[:, cols(t * DC, DC)] = total.astype(BF)
            return
        for half in (0, 1):
            first, second = AXES[half]
            along = lambda place: (place, slice(None)) if first == 0 else (slice(None), place)
            for sub in (0, 1):
                rows = self.rows(half, sub)
                if k == 1:
                    self.s1[half, sub, :, rows] = self.both(slot, *along(me.ring(first, 2)), half, sub).astype(BF)
                if k == 2:
                    for way, by in WAYS:
                        term = self.both(slot, *along(me.ring(first, by)), half, sub)
                        if sub == way:
                            term = term + self.r2[two, half, sub, :, rows].astype(F32)
                        self.s2[half, way, sub, :, rows] = term.astype(BF)
                if k == 3:
                    term = self.both(slot, *along(me.pos[first]), half, sub)
                    for way in (0, 1):
                        term = term + self.r3[two, half, way, sub, :, rows].astype(F32)
                    self.acc[two, half, sub, :, rows] = term
                    self.s4[half, sub, rows] = self.acc[two, half, sub, me.ring(second, 2), rows].astype(BF)
                if k == 4:
                    for way, by in WAYS:
                        term = self.acc[two, half, sub, me.ring(second, by), rows]
                        if sub == way:
                            term = term + self.r4[two, half, sub, rows].astype(F32)
                        self.s5[half, way, sub, rows] = term.astype(BF)
                if k == 5:
                    term = self.acc[two, half, sub, me.pos[second], rows]
                    for way in (0, 1):
                        term = term + self.r5[two, half, way, sub, rows].astype(F32)
                    lead, where, columns = self.part(half, sub)
                    if self.kind == "gu":
                        self.xb[two, me.x, lead, where, columns] = term.astype(BF)
                    else:
                        self.xb[two, me.x, where, columns] = term.astype(BF)

    def send(self, k, t, source=None):
        me, slot, two = self.me, lax.rem(t, self.big), lax.rem(t, SMALL)

        def go(src, dst, peer):
            pltpu.make_async_remote_copy(
                src_ref=src, dst_ref=dst, send_sem=self.ssem.at[k, slot], recv_sem=self.rsem.at[k, slot], device_id=peer, device_id_type=MESH
            ).start()

        if k == 0:
            go(source, self.inbox.at[slot], me.partner())
        if k == 5:
            for by in (1, 2, 3):
                go(self.xb.at[two, me.x], self.xb.at[two, me.x], me.across(by))
        for half in (0, 1):
            first, second = AXES[half]
            for way, by in WAYS:
                if k == 1:
                    rows = self.rows(half, way)
                    go(self.s1.at[half, way, :, rows], self.r2.at[two, half, way, :, rows], me.near(first, by))
                if k == 3:
                    rows = self.rows(half, way)
                    go(self.s4.at[half, way, rows], self.r4.at[two, half, way, rows], me.near(second, by))
                if k in (2, 4):
                    for sub in self.subs:
                        rows = self.rows(half, sub)
                        if k == 2:
                            go(self.s2.at[half, way, sub, :, rows], self.r3.at[two, half, way, sub, :, rows], me.near(first, by))
                        else:
                            go(self.s5.at[half, way, sub, rows], self.r5.at[two, half, way, sub, rows], me.near(second, by))


def stage_buffers(kind):
    block, last = ((2, NY, NZ, RD, TF), (2, RD, TF)) if kind == "gu" else ((NY, NZ, RF, DC), (RF, DC))
    big, piece, halves = BIG[kind], (40, 128), (2, 2)
    many = (4, *piece)
    vmem, sems = lambda *dims: pltpu.VMEM(dims, BF), pltpu.SemaphoreType.DMA
    return [
        vmem(big, 2, NY, NZ, 2, RD, TF) if kind == "gu" else vmem(big, *block),
        vmem(big, *block),
        vmem(*halves, *many),
        vmem(SMALL, *halves, *many),
        vmem(2, *halves, *many),
        vmem(SMALL, 2, *halves, *many),
        pltpu.VMEM((SMALL, *halves, *many), F32),
        vmem(*halves, *piece),
        vmem(SMALL, *halves, *piece),
        vmem(2, *halves, *piece),
        vmem(SMALL, 2, *halves, *piece),
        vmem(SMALL, NX, *last),
        sems((6, big)),
        sems((6, big)),
    ]


NBUF = 14


def back_kernel(with_da, *refs):
    refs = list(refs)
    take = lambda n: [refs.pop(0) for _ in range(n)]
    a, dy_in, wd, gate, up, dwd = take(6)
    if with_da:
        wgu, h, act = take(3)
        out_gu, out_d, dh, dwd_next = take(4)
    else:
        out_gu, out_d = take(2)
    gu_bufs, d_bufs = take(NBUF), take(NBUF)
    dg_s, du_s, lsem = take(3)
    dy = dy_in
    if with_da:
        da, dy, dsem = take(3)
    i = pl.program_id(0)
    me = Place()
    bring = pltpu.make_async_copy(dy_in, dy, dsem.at[0]) if with_da else None
    save = pltpu.make_async_copy(dy, dh, dsem.at[1]) if with_da else None

    @pl.when(i == 0)
    def _():
        if with_da:
            bring.start()
        me.meet(True)
        if with_da:
            bring.wait()

    own = gu_bufs[0]
    gu = Summing("gu", NT, me, *gu_bufs, out_gu)
    down = Summing("d", NDC, me, *d_bufs, out_d)

    def load(n):
        slot = lax.rem(n, down.big)
        return pltpu.make_async_copy(dwd.at[:, :, me.c, :, cols(n * DC, DC)], down.own.at[slot], lsem.at[slot])

    for k in (6, 5, 4, 3, 2, 1):
        for engine in (gu, down):
            t, there = engine.due(i, k)

            @pl.when(there)
            def _(k=k, engine=engine, t=t):
                if k == 1 and engine is down:
                    load(t).wait()
                engine.compute(k, t)

    for k in (5, 4, 3, 2, 1, 0):
        for engine in (gu, down):
            t, there = engine.due(i, k)

            @pl.when(there)
            def _(k=k, engine=engine, t=t):
                source = None
                if k == 0:
                    source = own.at[lax.rem(t, gu.big), :, :, :, 1 - me.c] if engine is gu else dwd.at[:, :, 1 - me.c, :, cols(t * DC, DC)]
                engine.send(k, t, source)

    @pl.when((i < NDC * down.stride) & (lax.rem(i, down.stride) == 0))
    def _():
        load(lax.div(i, down.stride)).start()

    @pl.when(i < NT)
    def _():
        slot = lax.rem(i, gu.big)
        rows = TOKENS // 4
        for r in range(4):
            part = pl.ds(r * rows, rows)
            dh = dot(dy[part, :], wd[...], 1, 1).astype(BF).astype(F32)
            g, u = gate[part, :], up[part, :]
            sg = jax.nn.sigmoid(g)
            du_s[part, :] = (dh * (g * sg)).astype(BF)
            dg_s[part, :] = (dh * u * (sg * (1 + g * (1 - sg)))).astype(BF)
        own[slot, 0] = dot(a[...], dg_s[...], 0, 0).reshape(NY, NZ, 2, RD, TF).astype(BF)
        own[slot, 1] = dot(a[...], du_s[...], 0, 0).reshape(NY, NZ, 2, RD, TF).astype(BF)
        if with_da:
            more = dot(dg_s[...], wgu[0], 1, 1) + dot(du_s[...], wgu[1], 1, 1)

            @pl.when(i == 0)
            def _():
                da[...] = more

            @pl.when(i > 0)
            def _():
                da[...] += more

    if not with_da:
        return

    @pl.when((i >= NT) & (i < NT + NR))
    def _():
        rows = TOKENS // NR
        part = pl.ds(pl.multiple_of((i - NT) * rows, rows), rows)
        wide, by_a = h[...].astype(F32), da[part, :].astype(BF).astype(F32)
        scale = lax.rsqrt(jnp.mean(wide**2, -1, keepdims=True) + 1e-6)
        by_h = by_a * scale - wide * (scale * scale * scale * jnp.mean(by_a * wide, -1, keepdims=True))
        dy[part, :] = dy[part, :] + by_h.astype(BF)

    @pl.when(i == NT + NR)
    def _():
        save.start()

    tiles = (dg_s, du_s)

    def bring_act(t, slot):
        return pltpu.make_async_copy(act.at[:, cols(t * TF, TF)], tiles[slot], dsem.at[2 + slot])

    @pl.when(i == NT + NR - 1)
    def _():
        bring_act(0, 0).start()

    t = i - NT - NR
    for slot in (0, 1):

        @pl.when((t >= 0) & (lax.rem(t, 2) == slot))
        def _(slot=slot):
            bring_act(t, slot).wait()

            @pl.when(t < NT - 1)
            def _():
                bring_act(t + 1, 1 - slot).start()

            dwd_next[...] = dot(tiles[slot][...], dy[...], 0, 0).astype(BF)

    @pl.when(i == pl.num_programs(0) - 1)
    def _():
        save.wait()


def backward(a, dy, g_d, gate, up, dwd, more, number):
    with_da = more is not None
    vmem, hbm = pl.BlockSpec(memory_space=pltpu.VMEM), pl.BlockSpec(memory_space=pl.ANY)
    shape, sems = jax.ShapeDtypeStruct, pltpu.SemaphoreType.DMA
    tile = pl.BlockSpec((TOKENS, TF), lambda i: (0, upto(i, NT - 1)))
    in_specs = [vmem, hbm if with_da else vmem, pl.BlockSpec((TF, D), lambda i: (upto(i, NT - 1), 0)), tile, tile, hbm]
    out_specs, out_shape = [vmem, vmem], [shape((2, RD, FF), BF), shape((RF, D), BF)]
    scratch = []
    if with_da:
        late = lambda i: above(i - NT - NR)
        in_specs += [
            pl.BlockSpec((2, D, TF), lambda i: (0, 0, upto(i, NT - 1))),
            pl.BlockSpec((TOKENS // NR, D), lambda i: (upto(above(i - NT), NR - 1), 0)),
            hbm,
        ]
        out_specs += [hbm, pl.BlockSpec((TF, D), lambda i: (late(i), 0))]
        out_shape += [shape((TOKENS, D), BF), shape((FF, D), BF)]
        scratch = [pltpu.VMEM((TOKENS, D), F32), pltpu.VMEM((TOKENS, D), BF), sems((4,))]
    return pl.pallas_call(
        functools.partial(back_kernel, with_da),
        grid=(2 * NT + NR if with_da else NT + STAGES,),
        in_specs=in_specs,
        out_specs=out_specs,
        out_shape=out_shape,
        scratch_shapes=[
            *stage_buffers("gu"),
            *stage_buffers("d"),
            pltpu.VMEM((TOKENS, TF), BF),
            pltpu.VMEM((TOKENS, TF), BF),
            sems((BIG["d"],)),
            *scratch,
        ],
        compiler_params=pltpu.CompilerParams(
            collective_id=number, has_side_effects=True, vmem_limit_bytes=VMEM_LIMIT, dimension_semantics=("arbitrary",)
        ),
        cost_estimate=pl.CostEstimate(
            flops=(12 if with_da else 6) * TOKENS * D * FF, bytes_accessed=200_000_000, transcendentals=TOKENS * FF
        ),
        name=f"backward_{number}",
    )(a, dy, g_d, gate, up, dwd.reshape(NY, NZ, 2, RF, D), *(more or ()))


def total_kernel(part, out, b0, b1, b2, ssem, rsem):
    me = Place()
    barrier = pltpu.get_barrier_semaphore()
    rings = [[me.near(axis, by) for by in (1, 2, 3)] for axis in (0, 1)] + [[me.partner()]]
    peers = [peer for ring in rings for peer in ring]
    for peer in peers:
        pl.semaphore_signal(barrier, inc=1, device_id=peer, device_id_type=MESH)
    pl.semaphore_wait(barrier, len(peers))
    value = part[...]
    for k, (buf, place, ring) in enumerate(zip((b0, b1, b2), (me.y, me.z, me.c), rings, strict=True)):
        buf[place] = value
        for peer in ring:
            pltpu.make_async_remote_copy(
                src_ref=buf.at[place], dst_ref=buf.at[place], send_sem=ssem.at[k], recv_sem=rsem.at[k], device_id=peer, device_id_type=MESH
            ).start()
        wait_bytes(buf.at[pl.ds(0, len(ring))], rsem.at[k])
        wait_bytes(buf.at[pl.ds(0, len(ring))], ssem.at[k])
        value = buf[0]
        for n in range(1, len(ring) + 1):
            value = value + buf[n]
    out[...] = value


def over_group(number, collective):
    part = jnp.full((8, 128), number, F32)
    vmem = pl.BlockSpec(memory_space=pltpu.VMEM)
    out = pl.pallas_call(
        total_kernel,
        in_specs=[vmem],
        out_specs=vmem,
        out_shape=jax.ShapeDtypeStruct((8, 128), F32),
        scratch_shapes=[
            pltpu.VMEM((NY, 8, 128), F32),
            pltpu.VMEM((NZ, 8, 128), F32),
            pltpu.VMEM((2, 8, 128), F32),
            pltpu.SemaphoreType.DMA((3,)),
            pltpu.SemaphoreType.DMA((3,)),
        ],
        compiler_params=pltpu.CompilerParams(collective_id=collective, has_side_effects=True),
        name="total",
    )(part)
    return out[0, 0]


def normed(h):
    wide = h.astype(F32)
    scale = lax.rsqrt(jnp.mean(wide**2, -1, keepdims=True) + 1e-6)
    return (wide * scale).astype(BF)


def adamw(w, m, v, g):
    m = 0.9 * m + 0.1 * g
    v = 0.95 * v + 0.05 * g * g
    step = m * lax.rsqrt(v + 1e-8) + 0.1 * w
    return (w - 0.02 * step).astype(BF), m, v


def clipped(gradients, sum_of_squares, count):
    factor = jnp.minimum(1.0, 0.5 * lax.rsqrt(sum_of_squares / count + 1e-30))
    return [g * factor for g in gradients]


def solution(mesh):
    def step(x, dy, *arrays):
        weights, m, v = (arrays[i : i + 3] for i in (0, 3, 6))
        shards = lambda layer: (jnp.stack([weights[0][layer], weights[1][layer]]), weights[2][layer])
        h0, dy = x[0], dy[0]
        _, d0, a0, act0, gate0, up0, h1 = gathered(h0, *shards(0), None, 0)
        gu1, d1, a1, gate1, up1, by_d1 = gathered(h1, *shards(1), dy, 1)
        mine_gu1, mine_d1, dh, by_d0 = backward(a1, dy, d1, gate1, up1, by_d1, (gu1, h1, act0), 2)
        mine_gu0, mine_d0 = backward(a0, dh, d0, gate0, up0, by_d0, None, 3)
        gradients = [jnp.stack([mine_gu0[n], mine_gu1[n]]).astype(F32) for n in (0, 1)] + [jnp.stack([mine_d0, mine_d1]).astype(F32)]
        squares = over_group(sum(jnp.sum(g * g) for g in gradients), 4)
        gradients = clipped(gradients, squares, S * sum(g.size for g in gradients))
        new = [adamw(w.astype(F32), m, v, g) for w, m, v, g in zip(weights, m, v, gradients, strict=True)]
        return tuple(one[which] for which in range(3) for one in new)

    states, cut = P(("rep", "r", "s"), None, None), P(None, "s", None)
    return jax.shard_map(
        step,
        mesh=mesh,
        in_specs=(states, states) + (cut,) * 9,
        out_specs=(P("rep", "s", None),) * 9,
        check_vma=False,
    )
```

time: 867 us -> 754 us (0.87); the launches traced: 870 us -> 746 us
  Pallas kernels: 779 us -> 721 us
  matrix products: 34.5 us -> 0 us
  other arithmetic: 40.9 us -> 14.5 us
    pallas_call x4, Pallas kernels: 763 us -> 703 us  [the longest x2 420 us: backward(): pl.pallas_call(functools.partial(back_kernel, with_da), grid=(2 * NT + NR...]
    dot_general x1 -> x0, matrix products: 34.5 us -> none  [dot(): lax.dot_general(a, b, (((ca,), (cb,)), ((), ())), preferred_element_type=...]
    reduce_sum x3 -> x0, other arithmetic: 14.2 us -> none  [the longest x2 7.45 us: normed(): scale = lax.rsqrt(jnp.mean(wide ** 2, -1, keepdims=True) + 1e-06)]
where the time goes in v3:
time: 754 us; the launch traced here: 746 us
  Pallas kernels  721 us (96%)
  other arithmetic  14.5 us (2%)
    pallas_call x2, Pallas kernels, backward(): pl.pallas_call(functools.partial(back_kernel, with_da), grid=(2 * NT + NR...  420 us
    pallas_call x2, Pallas kernels, gathered(): pl.pallas_call(functools.partial(gather_kernel, forward), grid=(LEAD + NT...  283 us
    pallas_call x1, Pallas kernels, over_group(): pl.pallas_call(total_kernel, in_specs=[vmem], out_specs=vmem, out_shape=j...  17.7 us

profile of v3, /device:TPU:1, one launch (start us, length us, event | category | flops | bytes accessed | tf_op | source)
XLA Modules:
  0.0 745.8 jit_solution(5298253247740259858)
XLA Ops:
  0.7 1.2 fusion.29
  1.9 0.1 copy-done.3
  2.0 0.1 fusion.30
  2.1 1.3 pad_maximum_fusion
  3.4 0.9 slice_bitcast_fusion
  4.3 147.8 %gather_0.1 = (bf16[2,4,4,2,40,4864]{5,4,3,2,1,0:T(8,128)(2,1)}, bf16[4,4,2,152,1280]{4,3,2,1,0:T(8,128)(2,1)}, bf16[2048,1280]{1,0:T(8,128)(2,1)}, bf16[2048,48...) custom-call(bf16[2048,1280]{1,0:T(8,128)(2,1)} %bitcast.18, ...), custom_call_target="tpu_custom_call" | custom-call | flops 76504104960 | bytes 200000000 | tf_op jit(solution)/shard_map/gather_0/pallas_call | solution.py:276
  152.1 134.9 %gather_1.1 = (bf16[2,4,4,2,40,4864]{5,4,3,2,1,0:T(8,128)(2,1)}, bf16[4,4,2,152,1280]{4,3,2,1,0:T(8,128)(2,1)}, bf16[2048,1280]{1,0:T(8,128)(2,1)}, f32[2048,486...) custom-call(bf16[2048,1280]{1,0:T(8,128)(2,1)} %get-tuple-element.28.refs_0_.refs_7_, ...), custom_call_target="tpu_custom_call" | custom-call | flops 76504104960 | bytes 200000000 | tf_op jit(solution)/shard_map/gather_1/pallas_call | solution.py:276
  287.0 264.6 %backward_2.1 = (bf16[2,40,4864]{2,1,0:T(8,128)(2,1)}, bf16[152,1280]{1,0:T(8,128)(2,1)}, bf16[2048,1280]{1,0:T(8,128)(2,1)}, bf16[4864,1280]{1,0:T(8,128)(2,1)}) custom-call(bf16[2048,1280]{1,0:T(8,128)(2,1)} %get-tuple-element.29.refs_0_, bf16[2048,1280]{1,0:T(8,128)(2,1)} %bitcast.20, bf16[4864,1280]{1,0:T(8,128)(2,1)} %bitcast.24, ...), custom_call_target="tpu_custom_call" | custom-call | flops 153008209920 | bytes 200000000 | tf_op jit(solution)/shard_map/backward_2/pallas_call | solution.py:603
  551.6 155.8 %backward_3.1 = (bf16[2,40,4864]{2,1,0:T(8,128)(2,1)}, bf16[152,1280]{1,0:T(8,128)(2,1)}) custom-call(bf16[2048,1280]{1,0:T(8,128)(2,1)} %get-tuple-element.27.refs_0_, bf16[2048,1280]{1,0:T(8,128)(2,1)} %get-tuple-element.36.refs_1_, bf16[4864,1280]{1,0:T(8,128)(2,1)} %bitcast.22, f32[2048,4864]{1,0:T(8,128)} %get-tuple-element.38.refs_3_, ...), custom_call_target="tpu_custom_call" | custom-call | flops 76504104960 | bytes 200000000 | tf_op jit(solution)/shard_map/backward_3/pallas_call | solution.py:603
  707.5 2.2 fusion.11
  709.6 1.2 fusion.27
  710.9 0.1 fusion.28
  710.9 1.0 fusion.9
  711.9 1.0 fusion.10
  714.9 0.6 broadcast_in_dim.3.part
  715.5 17.7 %total.1 = f32[8,128]{1,0:T(8,128)} custom-call(f32[8,128]{1,0:T(8,128)} %broadcast_in_dim.3.part), custom_call_target="tpu_custom_call" | custom-call | tf_op jit(solution)/shard_map/total/pallas_call | solution.py:653
  733.2 1.2 slice.43
  735.1 0.0 copy-start.8
  735.2 4.3 fusion.17
  739.5 0.0 copy-start.4
  739.5 2.3 fusion.8
  741.9 0.0 copy-done.9
  741.9 1.1 copy-done.10
  743.0 2.3 fusion.14
  (19 shorter events, 0.1 us)
Async XLA Ops:
  0.6 1.4 copy-start.3
  2.1 1.3 copy-start
  707.4 3.4 copy-start.11
  710.8 24.3 %copy-start.1 = (bf16[2,152,1280]{2,1,0:T(8,128)(2,1)S(1)}, bf16[2,152,1280]{2,1,0:T(8,128)(2,1)}, u32[]{:S(2)}) copy-start(bf16[2,152,1280]{2,1,0:T(8,128)(2,1)} %param.15) | copy-start | bytes 2334724
  710.8 24.3 %copy-start.5 = (bf16[152,1280]{1,0:T(8,128)(2,1)S(1)}, bf16[152,1280]{1,0:T(8,128)(2,1)}, u32[]{:S(2)}) copy-start(bf16[152,1280]{1,0:T(8,128)(2,1)} %get-tuple-element.44) | copy-start | bytes 1167364
  710.8 24.3 %copy-start.6 = (bf16[152,1280]{1,0:T(8,128)(2,1)S(1)}, bf16[152,1280]{1,0:T(8,128)(2,1)}, u32[]{:S(2)}) copy-start(bf16[152,1280]{1,0:T(8,128)(2,1)} %get-tuple-element.43) | copy-start | bytes 1167364
  735.1 4.4 copy-start.2
  735.1 4.4 copy-start.7
  735.1 4.4 copy-start.8
  739.5 2.4 copy-start.4
  739.5 2.4 copy-start.9
  739.5 3.5 copy-start.10

commit v4 on v3

--- a/solution.py
+++ b/solution.py
@@ -16,10 +16,12 @@
 S = NY * NZ * 2
 RD, RF = D // S, FF // S
 TF = 256
+HALF = TOKENS // 2
 NT = FF // TF
 ND = D // TF
 VMEM_LIMIT = 67_000_000
 AXES = ((0, 1), (1, 0))
+OTHERS = (1, 2, 3)
 WAYS = ((0, 1), (1, 3))
 
 
@@ -67,7 +69,7 @@
         barrier = pltpu.get_barrier_semaphore()
         peers = [self.near(axis, by) for axis in (0, 1) for by in (1, 3)] + [self.partner()]
         if x_too:
-            peers += [self.across(by) for by in (1, 2, 3)]
+            peers += [self.across(by) for by in OTHERS]
         for peer in peers:
             pl.semaphore_signal(barrier, inc=1, device_id=peer, device_id_type=MESH)
         pl.semaphore_wait(barrier, len(peers))
@@ -80,26 +82,32 @@
 CH = NT + 2
 LAG = 2
 LEAD = 5 * LAG + 1
+EARLY = 6
+LEAD_NEXT = LEAD - EARLY
+EARLY_AT = NT + 2 * ND - EARLY - 5 * LAG
 STAGES = 7
 ALONG_X = (-7, -5, -3, -1, 1, 9, 13, NT - 1)
+ALONG_X_NEXT = (-4, -2, 0, 2, 4, 12, 16, NT - 1)
 WITHIN = (3, 5, 7, 9, None, None, 11, NT - 1)
 
 
 def gather_kernel(forward, *refs):
     if forward:
-        h, wgu, wd, g_gu, g_d, a_out, act, gate, up, h_new, wt, wdt, act_s, a, ssem, rsem, lsem, osem = refs
+        h, wgu, wd, wgu_next, g_gu, g_d, a_out, act, gate, up, h_new, g_next, wt, wdt, act_s, a, ssem, rsem, lsem, osem = refs
+        lead, start_at, along_x = LEAD, 0, ALONG_X
     else:
-        h, wgu, wd, dy, g_gu, g_d, a_out, gate, up, dwd, wt, act_s, a, ssem, rsem, lsem, osem = refs
+        h, wgu, wd, dy, _, g_gu, g_d, a_out, gate, up, dwd, wt, act_s, a, ssem, rsem, lsem, osem = refs
+        lead, start_at, along_x = LEAD_NEXT, EARLY, ALONG_X_NEXT
     step = pl.program_id(0)
-    i = step - LEAD
+    i = step - lead
     me = Place()
+    whole = {"gu": (g_gu, wgu), "next": (g_next, wgu_next)} if forward else {"gu": (g_gu, wgu)}
     own = [
-        pltpu.make_async_copy(wgu, g_gu.at[:, me.y, me.z, me.c], osem.at[0]),
-        *(
-            pltpu.make_async_copy(wd.at[:, cols(t * TF, TF)], g_d.at[me.y, me.z, me.c, :, cols(t * TF, TF)], osem.at[n])
-            for n, t in ((1, me.x), (2, ND - 1))
-        ),
+        pltpu.make_async_copy(wd.at[:, cols(t * TF, TF)], g_d.at[me.y, me.z, me.c, :, cols(t * TF, TF)], osem.at[n])
+        for n, t in enumerate((me.x, ND - 1))
     ]
+    if forward:
+        own += [pltpu.make_async_copy(src, dst.at[:, me.y, me.z, me.c], osem.at[2 + n]) for n, (dst, src) in enumerate(whole.values())]
 
     @pl.when(step == 0)
     def _():
@@ -115,15 +123,15 @@
     def block(kind, t, half, sub, y, z, c):
         width = TF if half is None else TF // 2
         start = t * TF + (half or 0) * (TF // 2)
-        if kind == "gu":
+        if kind in whole:
             lead = slice(None) if sub is None else sub
-            return g_gu.at[lead, y, z, c, :, cols(start, width)]
+            return whole[kind][0].at[lead, y, z, c, :, cols(start, width)]
         rows = {None: slice(None), 0: pl.ds(0, 80), 1: pl.ds(80, RF - 80)}[sub]
         return g_d.at[y, z, c, rows, cols(start, width)]
 
     def mine(kind, t, half):
         start = t * TF + half * (TF // 2)
-        return wgu.at[:, :, cols(start, TF // 2)] if kind == "gu" else wd.at[:, cols(start, TF // 2)]
+        return whole[kind][1].at[:, :, cols(start, TF // 2)] if kind in whole else wd.at[:, cols(start, TF // 2)]
 
     ALL = slice(None)
 
@@ -184,7 +192,7 @@
 
     PLANE = (0, 1, 2, 3, 6)
 
-    save = pltpu.make_async_copy(a, a_out, osem.at[3])
+    save = pltpu.make_async_copy(a, a_out, osem.at[4])
 
     @pl.when(step == 1)
     def _():
@@ -197,19 +205,35 @@
     def _():
         save.start()
 
-    for n in (5, 4, 3, 2, 1, 0):
+    for n in reversed(range(6)):
         t = i + 1 + (5 - n) * LAG
 
-        @pl.when((t >= 0) & (t < NT))
+        @pl.when((t >= start_at) & (t < NT))
         def _(n=n, t=t):
             if n > 0:
                 wait_bytes(totals("gu", t, PLANE[n - 1]), rsem.at[PLANE[n - 1], t])
             if n < 5:
                 send("gu", t, t, PLANE[n])
-            else:
+
+        if n == 5:
+
+            @pl.when((t >= 0) & (t < NT))
+            def _(t=t):
                 load("gu", t).start()
 
-    for kind, t, ch, due in (("x", me.x, NT, ALONG_X), ("d", ND - 1, NT + 1, WITHIN)):
+    if forward:
+        for n in reversed(range(6)):
+            t = i - EARLY_AT - n * LAG
+
+            @pl.when((t >= 0) & (t < EARLY))
+            def _(n=n, t=t):
+                if n > 0:
+                    wait_bytes(totals("next", t, PLANE[n - 1]), rsem.at[PLANE[n - 1], CH + t])
+                if n < 5:
+                    send("next", t, CH + t, PLANE[n])
+
+    late = (("x", me.x, NT, along_x), ("d", ND - 1, NT + 1, WITHIN))
+    for kind, t, ch, due in late:
         stages = [k for k in range(STAGES + 1) if due[k] is not None]
         for before, k in zip([None, *stages], stages):
 
@@ -222,9 +246,16 @@
 
     if forward:
 
-        @pl.when((i >= NT - 1) & (i < NT + ND - 1))
+        j = i - NT
+        column, lower = lax.div(j, 2), lax.rem(j, 2)
+
+        @pl.when(i == NT - 1)
         def _():
-            load("d", i - NT + 1).start()
+            load("d", 0).start()
+
+        @pl.when((j >= 0) & (lower == 0) & (column < ND - 1))
+        def _():
+            load("d", column + 1).start()
 
     @pl.when((i >= 0) & (i < NT))
     def _():
@@ -244,62 +275,73 @@
 
     if forward:
 
-        @pl.when(i >= NT)
+        @pl.when((j >= 0) & (lower == 0))
         def _():
-            load("d", i - NT).wait()
-            h_new[...] = h[:, cols((i - NT) * TF, TF)] + dot(act_s[...], wdt[lax.rem(i - NT, 2)].reshape(FF, TF), 1, 0).astype(BF)
+            load("d", column).wait()
+
+        @pl.when(j >= 0)
+        def _():
+            part = pl.ds(pl.multiple_of(lower * HALF, HALF), HALF)
+            new = dot(act_s[part, :], wdt[lax.rem(column, 2)].reshape(FF, TF), 1, 0).astype(BF)
+            h_new[...] = h[part, cols(column * TF, TF)] + new
 
     @pl.when(step == pl.num_programs(0) - 1)
     def _():
         save.wait()
         for k in PLANE:
 
-            @pl.loop(0, NT)
+            @pl.loop(start_at, NT)
             def _(t, k=k):
                 wait_bytes(totals("gu", t, k), ssem.at[k, t])
 
-        for kind, t, ch, due in (("x", me.x, NT, ALONG_X), ("d", ND - 1, NT + 1, WITHIN)):
+            if forward:
+
+                @pl.loop(0, EARLY)
+                def _(t, k=k):
+                    wait_bytes(totals("next", t, k), ssem.at[k, CH + t])
+
+        for kind, t, ch, due in late:
             for k in range(STAGES):
                 if due[k] is not None:
                     wait_bytes(totals(kind, t, k), ssem.at[k, ch])
 
 
-def gathered(h, wgu, wd, dy, number):
-    forward = dy is None
+def gathered(h, wgu, wd, other, number):
+    forward = number == 0
+    lead = LEAD if forward else LEAD_NEXT
     vmem, hbm = pl.BlockSpec(memory_space=pltpu.VMEM), pl.BlockSpec(memory_space=pl.ANY)
-    tile = pl.BlockSpec((TOKENS, TF), lambda step: (0, upto(above(step - LEAD), NT - 1)))
-    column = pl.BlockSpec((TOKENS, TF), lambda step: (0, above(step - LEAD - NT)))
-    row = pl.BlockSpec((TF, D), lambda step: (upto(above(step - LEAD), NT - 1), 0))
+    tile = pl.BlockSpec((TOKENS, TF), lambda step: (0, upto(above(step - lead), NT - 1)))
+    column = pl.BlockSpec((HALF, TF), lambda step: (above(step - lead - NT) % 2, above(step - lead - NT) // 2))
+    row = pl.BlockSpec((TF, D), lambda step: (upto(above(step - lead), NT - 1), 0))
     shape, sems = jax.ShapeDtypeStruct, pltpu.SemaphoreType.DMA
+    states, matrices = shape((TOKENS, D), BF), shape((2, NY, NZ, 2, RD, FF), BF)
     wide = [shape((TOKENS, FF), F32)] * 2
-    states = shape((TOKENS, D), BF)
-    g_gu, g_d, *rest = pl.pallas_call(
+    return pl.pallas_call(
         functools.partial(gather_kernel, forward),
-        grid=(LEAD + NT + (ND if forward else 0),),
-        in_specs=[vmem, vmem, vmem] + ([] if forward else [vmem]),
-        out_specs=[hbm, hbm, hbm, *([tile] * 3 + [column] if forward else [tile, tile, row])],
+        grid=(lead + NT + (2 * ND if forward else 0),),
+        in_specs=[vmem, vmem, vmem, vmem, *([] if forward else [hbm])],
+        out_specs=[hbm, hbm, hbm, *([tile, tile, tile, column, hbm] if forward else [tile, tile, row])],
         out_shape=[
-            shape((2, NY, NZ, 2, RD, FF), BF),
+            matrices,
             shape((NY, NZ, 2, RF, D), BF),
             states,
-            *([shape((TOKENS, FF), BF), *wide, states] if forward else [*wide, shape((FF, D), BF)]),
+            *([shape((TOKENS, FF), BF), *wide, states, matrices] if forward else [*wide, shape((FF, D), BF)]),
         ],
         scratch_shapes=[
             pltpu.VMEM((2, 2, NY, NZ, 2, RD, TF), BF),
             *([pltpu.VMEM((2, NY, NZ, 2, RF, TF), BF), pltpu.VMEM((TOKENS, FF), BF)] if forward else [pltpu.VMEM((TOKENS, TF), BF)]),
             pltpu.VMEM((TOKENS, D), BF),
-            sems((STAGES, CH)),
-            sems((STAGES, CH)),
+            sems((STAGES, CH + EARLY)),
+            sems((STAGES, CH + EARLY)),
             sems((2, 2)),
-            sems((4,)),
+            sems((5,)),
         ],
+        input_output_aliases={} if forward else {4: 0},
         compiler_params=pltpu.CompilerParams(
             collective_id=number, has_side_effects=True, vmem_limit_bytes=VMEM_LIMIT, dimension_semantics=("arbitrary",)
         ),
-        cost_estimate=pl.CostEstimate(flops=6 * TOKENS * D * FF, bytes_accessed=200_000_000, transcendentals=TOKENS * FF),
         name=f"gather_{number}",
-    )(h, wgu, wd, *([] if forward else [dy]))
-    return g_gu.reshape(2, D, FF), g_d.reshape(FF, D), *rest
+    )(h, wgu, wd, *other)
 
 
 DC = 128
@@ -409,7 +451,7 @@
         if k == 0:
             go(source, self.inbox.at[slot], me.partner())
         if k == 5:
-            for by in (1, 2, 3):
+            for by in OTHERS:
                 go(self.xb.at[two, me.x], self.xb.at[two, me.x], me.across(by))
         for half in (0, 1):
             first, second = AXES[half]
@@ -490,7 +532,7 @@
         slot = lax.rem(n, down.big)
         return pltpu.make_async_copy(dwd.at[:, :, me.c, :, cols(n * DC, DC)], down.own.at[slot], lsem.at[slot])
 
-    for k in (6, 5, 4, 3, 2, 1):
+    for k in range(6, 0, -1):
         for engine in (gu, down):
             t, there = engine.due(i, k)
 
@@ -500,7 +542,7 @@
                     load(t).wait()
                 engine.compute(k, t)
 
-    for k in (5, 4, 3, 2, 1, 0):
+    for k in reversed(range(6)):
         for engine in (gu, down):
             t, there = engine.due(i, k)
 
@@ -617,9 +659,6 @@
         compiler_params=pltpu.CompilerParams(
             collective_id=number, has_side_effects=True, vmem_limit_bytes=VMEM_LIMIT, dimension_semantics=("arbitrary",)
         ),
-        cost_estimate=pl.CostEstimate(
-            flops=(12 if with_da else 6) * TOKENS * D * FF, bytes_accessed=200_000_000, transcendentals=TOKENS * FF
-        ),
         name=f"backward_{number}",
     )(a, dy, g_d, gate, up, dwd.reshape(NY, NZ, 2, RF, D), *(more or ()))
 
@@ -627,7 +666,7 @@
 def total_kernel(part, out, b0, b1, b2, ssem, rsem):
     me = Place()
     barrier = pltpu.get_barrier_semaphore()
-    rings = [[me.near(axis, by) for by in (1, 2, 3)] for axis in (0, 1)] + [[me.partner()]]
+    rings = [[me.near(axis, by) for by in OTHERS] for axis in (0, 1)] + [[me.partner()]]
     peers = [peer for ring in rings for peer in ring]
     for peer in peers:
         pl.semaphore_signal(barrier, inc=1, device_id=peer, device_id_type=MESH)
@@ -689,10 +728,11 @@
 def solution(mesh):
     def step(x, dy, *arrays):
         weights, m, v = (arrays[i : i + 3] for i in (0, 3, 6))
-        shards = lambda layer: (jnp.stack([weights[0][layer], weights[1][layer]]), weights[2][layer])
+        gu = [jnp.stack([weights[0][layer], weights[1][layer]]) for layer in (0, 1)]
         h0, dy = x[0], dy[0]
-        _, d0, a0, act0, gate0, up0, h1 = gathered(h0, *shards(0), None, 0)
-        gu1, d1, a1, gate1, up1, by_d1 = gathered(h1, *shards(1), dy, 1)
+        _, d0, a0, act0, gate0, up0, h1, first = gathered(h0, gu[0], weights[2][0], [gu[1]], 0)
+        gu1, d1, a1, gate1, up1, by_d1 = gathered(h1, gu[1], weights[2][1], [dy, first], 1)
+        gu1, d0, d1 = gu1.reshape(2, D, FF), d0.reshape(FF, D), d1.reshape(FF, D)
         mine_gu1, mine_d1, dh, by_d0 = backward(a1, dy, d1, gate1, up1, by_d1, (gu1, h1, act0), 2)
         mine_gu0, mine_d0 = backward(a0, dh, d0, gate0, up0, by_d0, None, 3)
         gradients = [jnp.stack([mine_gu0[n], mine_gu1[n]]).astype(F32) for n in (0, 1)] + [jnp.stack([mine_d0, mine_d1]).astype(F32)]

time: 754 us -> 735 us (0.975)
  Pallas kernels: 721 us -> 704 us
    pallas_call x2, Pallas kernels: 283 us -> 268 us  [gathered(): pl.pallas_call(functools.partial(gather_kernel, forward), grid=(lead + NT...]
where the time goes in v4:
time: 735 us; the launch traced here: 729 us
  Pallas kernels  704 us (96%)
  other arithmetic  14.5 us (2%)
    pallas_call x2, Pallas kernels, backward(): pl.pallas_call(functools.partial(back_kernel, with_da), grid=(2 * NT + NR...  418 us
    pallas_call x2, Pallas kernels, gathered(): pl.pallas_call(functools.partial(gather_kernel, forward), grid=(lead + NT...  268 us
    pallas_call x1, Pallas kernels, over_group(): pl.pallas_call(total_kernel, in_specs=[vmem], out_specs=vmem, out_shape=j...  17.5 us

profile of v4, /device:TPU:1, one launch (start us, length us, event | category | flops | bytes accessed | tf_op | source)
XLA Modules:
  0.0 728.7 jit_solution(1202376293647497507)
XLA Ops:
  0.7 1.2 fusion.29
  1.9 0.1 copy-done.3
  2.0 0.1 fusion.30
  2.1 0.0 copy-start
  2.1 1.3 pad_maximum_fusion
  3.4 0.9 slice_bitcast_fusion
  4.3 152.7 %gather_0.1 = (bf16[2,4,4,2,40,4864]{5,4,3,2,1,0:T(8,128)(2,1)}, bf16[4,4,2,152,1280]{4,3,2,1,0:T(8,128)(2,1)}, bf16[2048,1280]{1,0:T(8,128)(2,1)}, bf16[2048,48...) custom-call(bf16[2048,1280]{1,0:T(8,128)(2,1)} %bitcast.21, ...), custom_call_target="tpu_custom_call" | custom-call | tf_op jit(solution)/shard_map/gather_0/pallas_call | solution.py:319
  157.0 115.4 %gather_1.1 = (bf16[2,4,4,2,40,4864]{5,4,3,2,1,0:T(8,128)(2,1)}, bf16[4,4,2,152,1280]{4,3,2,1,0:T(8,128)(2,1)}, bf16[2048,1280]{1,0:T(8,128)(2,1)}, f32[2048,486...) custom-call(bf16[2048,1280]{1,0:T(8,128)(2,1)} %get-tuple-element.29.refs_0_.re, ...), custom_call_target="tpu_custom_call", output_to_operand_aliasing={{0}: (4, {})} | custom-call | tf_op jit(solution)/shard_map/gather_1/pallas_call | solution.py:319
  272.3 262.3 %backward_2.1 = (bf16[2,40,4864]{2,1,0:T(8,128)(2,1)}, bf16[152,1280]{1,0:T(8,128)(2,1)}, bf16[2048,1280]{1,0:T(8,128)(2,1)}, bf16[4864,1280]{1,0:T(8,128)(2,1)}) custom-call(bf16[2048,1280]{1,0:T(8,128)(2,1)} %get-tuple-element.31.refs_0_, bf16[2048,1280]{1,0:T(8,128)(2,1)} %bitcast.16, bf16[4864,1280]{1,0:T(8,128)(2,1)} %bitcast.17, ...), custom_call_target="tpu_custom_call" | custom-call | tf_op jit(solution)/shard_map/backward_2/pallas_call | solution.py:645
  534.7 155.9 %backward_3.1 = (bf16[2,40,4864]{2,1,0:T(8,128)(2,1)}, bf16[152,1280]{1,0:T(8,128)(2,1)}) custom-call(bf16[2048,1280]{1,0:T(8,128)(2,1)} %get-tuple-element.28.refs_0_, bf16[2048,1280]{1,0:T(8,128)(2,1)} %get-tuple-element.38.refs_1_, bf16[4864,1280]{1,0:T(8,128)(2,1)} %bitcast.19, f32[2048,4864]{1,0:T(8,128)} %get-tuple-element.40.refs_3_, ...), custom_call_target="tpu_custom_call" | custom-call | tf_op jit(solution)/shard_map/backward_3/pallas_call | solution.py:645
  690.5 2.2 fusion.11
  692.7 1.2 fusion.27
  693.9 0.0 copy-start.1
  693.9 0.1 fusion.28
  694.0 1.0 fusion.9
  695.0 1.0 fusion.10
  697.9 0.6 broadcast_in_dim.3.part
  698.5 17.5 %total.1 = f32[8,128]{1,0:T(8,128)} custom-call(f32[8,128]{1,0:T(8,128)} %broadcast_in_dim.3.part), custom_call_target="tpu_custom_call" | custom-call | tf_op jit(solution)/shard_map/total/pallas_call | solution.py:692
  716.1 1.2 slice.43
  718.0 4.3 fusion.17
  722.4 2.3 fusion.8
  724.7 0.0 copy-done.9
  724.8 1.1 copy-done.10
  725.9 2.3 fusion.14
  (19 shorter events, 0.1 us)
Async XLA Ops:
  0.6 1.4 copy-start.3
  2.1 1.3 copy-start
  690.5 3.4 copy-start.11
  693.9 24.1 %copy-start.1 = (bf16[2,152,1280]{2,1,0:T(8,128)(2,1)S(1)}, bf16[2,152,1280]{2,1,0:T(8,128)(2,1)}, u32[]{:S(2)}) copy-start(bf16[2,152,1280]{2,1,0:T(8,128)(2,1)} %param.15) | copy-start | bytes 2334724
  693.9 24.1 %copy-start.5 = (bf16[152,1280]{1,0:T(8,128)(2,1)S(1)}, bf16[152,1280]{1,0:T(8,128)(2,1)}, u32[]{:S(2)}) copy-start(bf16[152,1280]{1,0:T(8,128)(2,1)} %get-tuple-element.46) | copy-start | bytes 1167364
  693.9 24.1 %copy-start.6 = (bf16[152,1280]{1,0:T(8,128)(2,1)S(1)}, bf16[152,1280]{1,0:T(8,128)(2,1)}, u32[]{:S(2)}) copy-start(bf16[152,1280]{1,0:T(8,128)(2,1)} %get-tuple-element.45) | copy-start | bytes 1167364
  718.0 4.4 copy-start.2
  718.0 4.4 copy-start.7
  718.0 4.4 copy-start.8
  722.4 2.4 copy-start.4
  722.4 2.4 copy-start.9
  722.4 3.5 copy-start.10

commit v5 on v4

--- a/solution.py
+++ b/solution.py
@@ -65,11 +65,13 @@
     def across(self, by):
         return {"r": lax.rem(self.x + by, NX)}
 
-    def meet(self, x_too):
+    def meet(self, x_too, far_too=False):
         barrier = pltpu.get_barrier_semaphore()
         peers = [self.near(axis, by) for axis in (0, 1) for by in (1, 3)] + [self.partner()]
         if x_too:
             peers += [self.across(by) for by in OTHERS]
+        if far_too:
+            peers += [self.near(axis, 2) for axis in (0, 1)]
         for peer in peers:
             pl.semaphore_signal(barrier, inc=1, device_id=peer, device_id_type=MESH)
         pl.semaphore_wait(barrier, len(peers))
@@ -88,16 +90,19 @@
 STAGES = 7
 ALONG_X = (-7, -5, -3, -1, 1, 9, 13, NT - 1)
 ALONG_X_NEXT = (-4, -2, 0, 2, 4, 12, 16, NT - 1)
-WITHIN = (3, 5, 7, 9, None, None, 11, NT - 1)
+WITHIN = (12, 14, 16, 18, None, None, 20, NT + 2 * ND - 4)
+WITHIN_NEXT = (3, 5, 7, 9, None, None, 11, NT - 1)
 
 
 def gather_kernel(forward, *refs):
     if forward:
-        h, wgu, wd, wgu_next, g_gu, g_d, a_out, act, gate, up, h_new, g_next, wt, wdt, act_s, a, ssem, rsem, lsem, osem = refs
-        lead, start_at, along_x = LEAD, 0, ALONG_X
+        h, shards, downs, g_gu, g_d, a_out, act, gate, up, h_new, g_next, wt, wdt, act_s, a, ssem, rsem, lsem, osem = refs
+        lead, start_at, along_x, within = LEAD, 0, ALONG_X, WITHIN
+        wgu, wd, wgu_next = shards.at[0], downs.at[0], shards.at[1]
     else:
-        h, wgu, wd, dy, _, g_gu, g_d, a_out, gate, up, dwd, wt, act_s, a, ssem, rsem, lsem, osem = refs
-        lead, start_at, along_x = LEAD_NEXT, EARLY, ALONG_X_NEXT
+        h, shards, downs, dy, _, g_gu, g_d, a_out, gate, up, dwd, wt, act_s, a, ssem, rsem, lsem, osem = refs
+        lead, start_at, along_x, within = LEAD_NEXT, EARLY, ALONG_X_NEXT, WITHIN_NEXT
+        wgu, wd = shards.at[1], downs.at[1]
     step = pl.program_id(0)
     i = step - lead
     me = Place()
@@ -232,7 +237,7 @@
                 if n < 5:
                     send("next", t, CH + t, PLANE[n])
 
-    late = (("x", me.x, NT, along_x), ("d", ND - 1, NT + 1, WITHIN))
+    late = (("x", me.x, NT, along_x), ("d", ND - 1, NT + 1, within))
     for kind, t, ch, due in late:
         stages = [k for k in range(STAGES + 1) if due[k] is not None]
         for before, k in zip([None, *stages], stages):
@@ -306,7 +311,7 @@
                     wait_bytes(totals(kind, t, k), ssem.at[k, ch])
 
 
-def gathered(h, wgu, wd, other, number):
+def gathered(h, shards, downs, other, number):
     forward = number == 0
     lead = LEAD if forward else LEAD_NEXT
     vmem, hbm = pl.BlockSpec(memory_space=pltpu.VMEM), pl.BlockSpec(memory_space=pl.ANY)
@@ -319,7 +324,7 @@
     return pl.pallas_call(
         functools.partial(gather_kernel, forward),
         grid=(lead + NT + (2 * ND if forward else 0),),
-        in_specs=[vmem, vmem, vmem, vmem, *([] if forward else [hbm])],
+        in_specs=[vmem, vmem, vmem, *([] if forward else [vmem, hbm])],
         out_specs=[hbm, hbm, hbm, *([tile, tile, tile, column, hbm] if forward else [tile, tile, row])],
         out_shape=[
             matrices,
@@ -341,7 +346,7 @@
             collective_id=number, has_side_effects=True, vmem_limit_bytes=VMEM_LIMIT, dimension_semantics=("arbitrary",)
         ),
         name=f"gather_{number}",
-    )(h, wgu, wd, *other)
+    )(h, shards, downs, *other)
 
 
 DC = 128
@@ -497,6 +502,22 @@
 NBUF = 14
 
 
+def sum_over_group(me, value, out, bufs, ssem, rsem):
+    rings = [[me.near(axis, by) for by in OTHERS] for axis in (0, 1)] + [[me.partner()]]
+    for k, (buf, place, ring) in enumerate(zip(bufs, (me.y, me.z, me.c), rings)):
+        buf[place] = value
+        for peer in ring:
+            pltpu.make_async_remote_copy(
+                src_ref=buf.at[place], dst_ref=buf.at[place], send_sem=ssem.at[k], recv_sem=rsem.at[k], device_id=peer, device_id_type=MESH
+            ).start()
+        wait_bytes(buf.at[pl.ds(0, len(ring))], rsem.at[k])
+        wait_bytes(buf.at[pl.ds(0, len(ring))], ssem.at[k])
+        value = buf[0]
+        for n in range(1, len(ring) + 1):
+            value = value + buf[n]
+    out[...] = value
+
+
 def back_kernel(with_da, *refs):
     refs = list(refs)
     take = lambda n: [refs.pop(0) for _ in range(n)]
@@ -505,12 +526,16 @@
         wgu, h, act = take(3)
         out_gu, out_d, dh, dwd_next = take(4)
     else:
-        out_gu, out_d = take(2)
+        parts = take(2)
+        out_gu, out_d, total = take(3)
     gu_bufs, d_bufs = take(NBUF), take(NBUF)
     dg_s, du_s, lsem = take(3)
     dy = dy_in
     if with_da:
         da, dy, dsem = take(3)
+    else:
+        rings = take(3)
+        tsems = take(2)
     i = pl.program_id(0)
     me = Place()
     bring = pltpu.make_async_copy(dy_in, dy, dsem.at[0]) if with_da else None
@@ -520,7 +545,7 @@
     def _():
         if with_da:
             bring.start()
-        me.meet(True)
+        me.meet(True, not with_da)
         if with_da:
             bring.wait()
 
@@ -582,6 +607,15 @@
                 da[...] += more
 
     if not with_da:
+
+        @pl.when(i == pl.num_programs(0) - 1)
+        def _():
+            squares = jnp.zeros((8, 128), F32)
+            for ref in (*parts, out_gu, out_d):
+                for block in (ref,) if len(ref.shape) == 2 else (ref.at[0], ref.at[1]):
+                    squares = squares + jnp.sum(block[...].astype(F32) ** 2)
+            sum_over_group(me, squares, total, rings, *tsems)
+
         return
 
     @pl.when((i >= NT) & (i < NT + NR))
@@ -625,7 +659,7 @@
 
 
 def backward(a, dy, g_d, gate, up, dwd, more, number):
-    with_da = more is not None
+    with_da = number == 2
     vmem, hbm = pl.BlockSpec(memory_space=pltpu.VMEM), pl.BlockSpec(memory_space=pl.ANY)
     shape, sems = jax.ShapeDtypeStruct, pltpu.SemaphoreType.DMA
     tile = pl.BlockSpec((TOKENS, TF), lambda i: (0, upto(i, NT - 1)))
@@ -642,6 +676,12 @@
         out_specs += [hbm, pl.BlockSpec((TF, D), lambda i: (late(i), 0))]
         out_shape += [shape((TOKENS, D), BF), shape((FF, D), BF)]
         scratch = [pltpu.VMEM((TOKENS, D), F32), pltpu.VMEM((TOKENS, D), BF), sems((4,))]
+    else:
+        tiny = (8, 128)
+        in_specs += [vmem, vmem]
+        out_specs += [vmem]
+        out_shape += [shape(tiny, F32)]
+        scratch = [*(pltpu.VMEM((n, *tiny), F32) for n in (NY, NZ, 2)), sems((3,)), sems((3,))]
     return pl.pallas_call(
         functools.partial(back_kernel, with_da),
         grid=(2 * NT + NR if with_da else NT + STAGES,),
@@ -660,51 +700,7 @@
             collective_id=number, has_side_effects=True, vmem_limit_bytes=VMEM_LIMIT, dimension_semantics=("arbitrary",)
         ),
         name=f"backward_{number}",
-    )(a, dy, g_d, gate, up, dwd.reshape(NY, NZ, 2, RF, D), *(more or ()))
-
-
-def total_kernel(part, out, b0, b1, b2, ssem, rsem):
-    me = Place()
-    barrier = pltpu.get_barrier_semaphore()
-    rings = [[me.near(axis, by) for by in OTHERS] for axis in (0, 1)] + [[me.partner()]]
-    peers = [peer for ring in rings for peer in ring]
-    for peer in peers:
-        pl.semaphore_signal(barrier, inc=1, device_id=peer, device_id_type=MESH)
-    pl.semaphore_wait(barrier, len(peers))
-    value = part[...]
-    for k, (buf, place, ring) in enumerate(zip((b0, b1, b2), (me.y, me.z, me.c), rings, strict=True)):
-        buf[place] = value
-        for peer in ring:
-            pltpu.make_async_remote_copy(
-                src_ref=buf.at[place], dst_ref=buf.at[place], send_sem=ssem.at[k], recv_sem=rsem.at[k], device_id=peer, device_id_type=MESH
-            ).start()
-        wait_bytes(buf.at[pl.ds(0, len(ring))], rsem.at[k])
-        wait_bytes(buf.at[pl.ds(0, len(ring))], ssem.at[k])
-        value = buf[0]
-        for n in range(1, len(ring) + 1):
-            value = value + buf[n]
-    out[...] = value
-
-
-def over_group(number, collective):
-    part = jnp.full((8, 128), number, F32)
-    vmem = pl.BlockSpec(memory_space=pltpu.VMEM)
-    out = pl.pallas_call(
-        total_kernel,
-        in_specs=[vmem],
-        out_specs=vmem,
-        out_shape=jax.ShapeDtypeStruct((8, 128), F32),
-        scratch_shapes=[
-            pltpu.VMEM((NY, 8, 128), F32),
-            pltpu.VMEM((NZ, 8, 128), F32),
-            pltpu.VMEM((2, 8, 128), F32),
-            pltpu.SemaphoreType.DMA((3,)),
-            pltpu.SemaphoreType.DMA((3,)),
-        ],
-        compiler_params=pltpu.CompilerParams(collective_id=collective, has_side_effects=True),
-        name="total",
-    )(part)
-    return out[0, 0]
+    )(a, dy, g_d, gate, up, dwd.reshape(NY, NZ, 2, RF, D), *more)
 
 
 def normed(h):
@@ -728,16 +724,15 @@
 def solution(mesh):
     def step(x, dy, *arrays):
         weights, m, v = (arrays[i : i + 3] for i in (0, 3, 6))
-        gu = [jnp.stack([weights[0][layer], weights[1][layer]]) for layer in (0, 1)]
+        shards = jnp.stack(weights[:2], 1), weights[2]
         h0, dy = x[0], dy[0]
-        _, d0, a0, act0, gate0, up0, h1, first = gathered(h0, gu[0], weights[2][0], [gu[1]], 0)
-        gu1, d1, a1, gate1, up1, by_d1 = gathered(h1, gu[1], weights[2][1], [dy, first], 1)
+        _, d0, a0, act0, gate0, up0, h1, first = gathered(h0, *shards, [], 0)
+        gu1, d1, a1, gate1, up1, by_d1 = gathered(h1, *shards, [dy, first], 1)
         gu1, d0, d1 = gu1.reshape(2, D, FF), d0.reshape(FF, D), d1.reshape(FF, D)
         mine_gu1, mine_d1, dh, by_d0 = backward(a1, dy, d1, gate1, up1, by_d1, (gu1, h1, act0), 2)
-        mine_gu0, mine_d0 = backward(a0, dh, d0, gate0, up0, by_d0, None, 3)
+        mine_gu0, mine_d0, squares = backward(a0, dh, d0, gate0, up0, by_d0, (mine_gu1, mine_d1), 3)
         gradients = [jnp.stack([mine_gu0[n], mine_gu1[n]]).astype(F32) for n in (0, 1)] + [jnp.stack([mine_d0, mine_d1]).astype(F32)]
-        squares = over_group(sum(jnp.sum(g * g) for g in gradients), 4)
-        gradients = clipped(gradients, squares, S * sum(g.size for g in gradients))
+        gradients = clipped(gradients, squares[0, 0], S * sum(g.size for g in gradients))
         new = [adamw(w.astype(F32), m, v, g) for w, m, v, g in zip(weights, m, v, gradients, strict=True)]
         return tuple(one[which] for which in range(3) for one in new)
 

time: 735 us -> 722 us (0.982)
    pallas_call x1 -> x0, Pallas kernels: 17.5 us -> none  [over_group(): pl.pallas_call(total_kernel, in_specs=[vmem], out_specs=vmem, out_shape=j...]
    pallas_call x2, Pallas kernels: 418 us -> 433 us  [backward(): pl.pallas_call(functools.partial(back_kernel, with_da), grid=(2 * NT + NR...]
where the time goes in v5:
time: 722 us; the launch traced here: 716 us
  Pallas kernels  700 us (97%)
  other arithmetic  10.6 us (1%)
    pallas_call x2, Pallas kernels, backward(): pl.pallas_call(functools.partial(back_kernel, with_da), grid=(2 * NT + NR...  433 us
    pallas_call x2, Pallas kernels, gathered(): pl.pallas_call(functools.partial(gather_kernel, forward), grid=(lead + NT...  266 us

profile of v5, /device:TPU:1, one launch (start us, length us, event | category | flops | bytes accessed | tf_op | source)
XLA Modules:
  0.0 716.1 jit_solution(16705978722699967986)
XLA Ops:
  0.6 2.6 pad_maximum_fusion.refs_1_
  3.3 149.1 %gather_0.1 = (bf16[2,4,4,2,40,4864]{5,4,3,2,1,0:T(8,128)(2,1)}, bf16[4,4,2,152,1280]{4,3,2,1,0:T(8,128)(2,1)}, bf16[2048,1280]{1,0:T(8,128)(2,1)}, bf16[2048,48...) custom-call(bf16[2048,1280]{1,0:T(8,128)(2,1)} %bitcast.19, ...), custom_call_target="tpu_custom_call" | custom-call | tf_op jit(solution)/shard_map/gather_0/pallas_call | solution.py:324
  152.4 117.0 %gather_1.1 = (bf16[2,4,4,2,40,4864]{5,4,3,2,1,0:T(8,128)(2,1)}, bf16[4,4,2,152,1280]{4,3,2,1,0:T(8,128)(2,1)}, bf16[2048,1280]{1,0:T(8,128)(2,1)}, f32[2048,486...) custom-call(bf16[2048,1280]{1,0:T(8,128)(2,1)} %get-tuple-element.30.refs_0_.re, ...), custom_call_target="tpu_custom_call", output_to_operand_aliasing={{0}: (4, {})} | custom-call | tf_op jit(solution)/shard_map/gather_1/pallas_call | solution.py:324
  269.4 262.4 %backward_2.1 = (bf16[2,40,4864]{2,1,0:T(8,128)(2,1)}, bf16[152,1280]{1,0:T(8,128)(2,1)}, bf16[2048,1280]{1,0:T(8,128)(2,1)}, bf16[4864,1280]{1,0:T(8,128)(2,1)}) custom-call(bf16[2048,1280]{1,0:T(8,128)(2,1)} %get-tuple-element.32.refs_0_, bf16[2048,1280]{1,0:T(8,128)(2,1)} %bitcast.14, bf16[4864,1280]{1,0:T(8,128)(2,1)} %bitcast.15, ...), custom_call_target="tpu_custom_call" | custom-call | tf_op jit(solution)/shard_map/backward_2/pallas_call | solution.py:685
  531.8 171.1 %backward_3.1 = (bf16[2,40,4864]{2,1,0:T(8,128)(2,1)}, bf16[152,1280]{1,0:T(8,128)(2,1)}, f32[8,128]{1,0:T(8,128)}) custom-call(bf16[2048,1280]{1,0:T(8,128)(2,1)} %get-tuple-element.29.refs_0_, bf16[2048,1280]{1,0:T(8,128)(2,1)} %get-tuple-element.39.refs_1_, bf16[4864,1280]{1,0:T(8,128)(2,1)} %bitcast.17, f32[2048,4864]{1,0:T(8,128)} %get-tuple-element.41.refs_3_, ...), custom_call_target="tpu_custom_call" | custom-call | tf_op jit(solution)/shard_map/backward_3/pallas_call | solution.py:685
  702.9 0.0 copy-start.1
  702.9 1.3 slice.17
  704.9 0.0 copy-start
  704.9 0.0 copy-start.4
  704.9 0.0 copy-start.9
  704.9 1.3 fusion.15
  706.2 0.0 copy-done.1
  706.2 0.1 fusion.16
  706.2 0.0 copy-done
  706.3 0.1 copy-done.4
  706.3 0.1 copy-done.9
  706.5 0.0 copy-start.7
  706.5 0.0 copy-start.8
  706.5 4.3 fusion.8
  710.8 0.0 copy-done.2
  710.8 0.0 copy-done.5
  710.8 0.3 copy-done.7
  711.1 0.9 copy-done.8
  712.1 3.6 fusion.2
  (6 shorter events, 0.0 us)
Async XLA Ops:
  702.9 3.3 copy-start.1
  704.9 1.4 copy-start
  704.9 1.5 copy-start.4
  704.9 1.6 copy-start.9
  706.4 4.4 copy-start.2
  706.4 4.4 copy-start.3
  706.4 4.4 copy-start.5
  706.4 4.4 copy-start.6
  706.5 4.7 copy-start.7
  706.5 5.6 copy-start.8

commit v6 on v5

--- a/solution.py
+++ b/solution.py
@@ -17,6 +17,7 @@
 RD, RF = D // S, FF // S
 TF = 256
 HALF = TOKENS // 2
+LANES = 128
 NT = FF // TF
 ND = D // TF
 VMEM_LIMIT = 67_000_000
@@ -42,7 +43,7 @@
 
 
 def cols(start, size):
-    return pl.ds(pl.multiple_of(start, 128), size)
+    return pl.ds(pl.multiple_of(start, LANES), size)
 
 
 class Place:
@@ -111,32 +112,39 @@
         pltpu.make_async_copy(wd.at[:, cols(t * TF, TF)], g_d.at[me.y, me.z, me.c, :, cols(t * TF, TF)], osem.at[n])
         for n, t in enumerate((me.x, ND - 1))
     ]
-    if forward:
-        own += [pltpu.make_async_copy(src, dst.at[:, me.y, me.z, me.c], osem.at[2 + n]) for n, (dst, src) in enumerate(whole.values())]
+
+    def own_tile(t, kind, sem):
+        dst, src = whole[kind]
+        return pltpu.make_async_copy(src.at[:, :, cols(t * TF, TF)], dst.at[t, :, me.y, me.z, me.c], sem)
 
     @pl.when(step == 0)
     def _():
         me.meet(True)
         for copy in own:
             copy.start()
+        if forward:
+            for n, kind in enumerate(whole):
+                pl.loop(0, NT)(lambda t, n=n, kind=kind: own_tile(t, kind, osem.at[2 + n]).start())
 
     @pl.when(step == 2 * LAG)
     def _():
         for copy in own:
             copy.wait()
+        if forward:
+            for n, (_, src) in enumerate(whole.values()):
+                wait_bytes(src, osem.at[2 + n])
 
     def block(kind, t, half, sub, y, z, c):
+        if kind in whole:
+            lead, columns = slice(None) if half is None else half, slice(None) if sub is None else cols(sub * LANES, LANES)
+            return whole[kind][0].at[t, lead, y, z, c, :, columns]
         width = TF if half is None else TF // 2
         start = t * TF + (half or 0) * (TF // 2)
-        if kind in whole:
-            lead = slice(None) if sub is None else sub
-            return whole[kind][0].at[lead, y, z, c, :, cols(start, width)]
         rows = {None: slice(None), 0: pl.ds(0, 80), 1: pl.ds(80, RF - 80)}[sub]
         return g_d.at[y, z, c, rows, cols(start, width)]
 
     def mine(kind, t, half):
-        start = t * TF + half * (TF // 2)
-        return whole[kind][1].at[:, :, cols(start, TF // 2)] if kind in whole else wd.at[:, cols(start, TF // 2)]
+        return whole[kind][1].at[half, :, cols(t * TF, TF)] if kind in whole else wd.at[:, cols(t * TF + half * LANES, LANES)]
 
     ALL = slice(None)
 
@@ -192,7 +200,7 @@
     def load(kind, t):
         slot = lax.rem(t, 2)
         if kind == "gu":
-            return pltpu.make_async_copy(g_gu.at[:, :, :, :, :, cols(t * TF, TF)], wt.at[slot], lsem.at[0, slot])
+            return pltpu.make_async_copy(g_gu.at[t], wt.at[slot], lsem.at[0, slot])
         return pltpu.make_async_copy(g_d.at[:, :, :, :, cols(t * TF, TF)], wdt.at[slot], lsem.at[1, slot])
 
     PLANE = (0, 1, 2, 3, 6)
@@ -319,7 +327,7 @@
     column = pl.BlockSpec((HALF, TF), lambda step: (above(step - lead - NT) % 2, above(step - lead - NT) // 2))
     row = pl.BlockSpec((TF, D), lambda step: (upto(above(step - lead), NT - 1), 0))
     shape, sems = jax.ShapeDtypeStruct, pltpu.SemaphoreType.DMA
-    states, matrices = shape((TOKENS, D), BF), shape((2, NY, NZ, 2, RD, FF), BF)
+    states, matrices = shape((TOKENS, D), BF), shape((NT, 2, NY, NZ, 2, RD, TF), BF)
     wide = [shape((TOKENS, FF), F32)] * 2
     return pl.pallas_call(
         functools.partial(gather_kernel, forward),
@@ -349,7 +357,7 @@
     )(h, shards, downs, *other)
 
 
-DC = 128
+DC = LANES
 STRIDE = {"gu": 1, "d": 2}
 BIG, SMALL = {"gu": 4, "d": 2}, 2
 NR = 8
@@ -374,7 +382,7 @@
 
     def part(self, half, sub):
         if self.kind == "gu":
-            return sub, slice(None), pl.ds(half * 128, 128)
+            return sub, slice(None), pl.ds(half * LANES, LANES)
         low = 80 * half + 40 * sub
         return 0, pl.ds(low, self.HEIGHTS["d"][half][sub]), slice(None)
 
@@ -478,7 +486,7 @@
 
 def stage_buffers(kind):
     block, last = ((2, NY, NZ, RD, TF), (2, RD, TF)) if kind == "gu" else ((NY, NZ, RF, DC), (RF, DC))
-    big, piece, halves = BIG[kind], (40, 128), (2, 2)
+    big, piece, halves = BIG[kind], (40, LANES), (2, 2)
     many = (4, *piece)
     vmem, sems = lambda *dims: pltpu.VMEM(dims, BF), pltpu.SemaphoreType.DMA
     return [
@@ -669,7 +677,7 @@
     if with_da:
         late = lambda i: above(i - NT - NR)
         in_specs += [
-            pl.BlockSpec((2, D, TF), lambda i: (0, 0, upto(i, NT - 1))),
+            pl.BlockSpec((None, 2, D, TF), lambda i: (upto(i, NT - 1), 0, 0, 0)),
             pl.BlockSpec((TOKENS // NR, D), lambda i: (upto(above(i - NT), NR - 1), 0)),
             hbm,
         ]
@@ -728,7 +736,7 @@
         h0, dy = x[0], dy[0]
         _, d0, a0, act0, gate0, up0, h1, first = gathered(h0, *shards, [], 0)
         gu1, d1, a1, gate1, up1, by_d1 = gathered(h1, *shards, [dy, first], 1)
-        gu1, d0, d1 = gu1.reshape(2, D, FF), d0.reshape(FF, D), d1.reshape(FF, D)
+        gu1, d0, d1 = gu1.reshape(NT, 2, D, TF), d0.reshape(FF, D), d1.reshape(FF, D)
         mine_gu1, mine_d1, dh, by_d0 = backward(a1, dy, d1, gate1, up1, by_d1, (gu1, h1, act0), 2)
         mine_gu0, mine_d0, squares = backward(a0, dh, d0, gate0, up0, by_d0, (mine_gu1, mine_d1), 3)
         gradients = [jnp.stack([mine_gu0[n], mine_gu1[n]]).astype(F32) for n in (0, 1)] + [jnp.stack([mine_d0, mine_d1]).astype(F32)]

time: 722 us -> 722 us (level)
  no operation moved by 1% of the time
where the time goes in v6:
time: 722 us; the launch traced here: 715 us
  Pallas kernels  699 us (97%)
  other arithmetic  10.6 us (1%)
    pallas_call x2, Pallas kernels, backward(): pl.pallas_call(functools.partial(back_kernel, with_da), grid=(2 * NT + NR...  433 us
    pallas_call x2, Pallas kernels, gathered(): pl.pallas_call(functools.partial(gather_kernel, forward), grid=(lead + NT...  266 us

profile of v6, /device:TPU:1, one launch (start us, length us, event | category | flops | bytes accessed | tf_op | source)
XLA Modules:
  0.0 715.4 jit_solution(14453988820649118951)
XLA Ops:
  0.6 2.6 pad_maximum_fusion.refs_1_
  3.3 149.5 %gather_0.1 = (bf16[19,2,4,4,2,40,256]{6,5,4,3,2,1,0:T(8,128)(2,1)}, bf16[4,4,2,152,1280]{4,3,2,1,0:T(8,128)(2,1)}, bf16[2048,1280]{1,0:T(8,128)(2,1)}, bf16[204...) custom-call(bf16[2048,1280]{1,0:T(8,128)(2,1)} %bitcast.19, ...), custom_call_target="tpu_custom_call" | custom-call | tf_op jit(solution)/shard_map/gather_0/pallas_call | solution.py:332
  152.8 116.6 %gather_1.1 = (bf16[19,2,4,4,2,40,256]{6,5,4,3,2,1,0:T(8,128)(2,1)}, bf16[4,4,2,152,1280]{4,3,2,1,0:T(8,128)(2,1)}, bf16[2048,1280]{1,0:T(8,128)(2,1)}, f32[2048...) custom-call(bf16[2048,1280]{1,0:T(8,128)(2,1)} %get-tuple-element.30.refs_0, ...), custom_call_target="tpu_custom_call", output_to_operand_aliasing={{0}: (4, {})} | custom-call | tf_op jit(solution)/shard_map/gather_1/pallas_call | solution.py:332
  269.4 261.2 %backward_2.1 = (bf16[2,40,4864]{2,1,0:T(8,128)(2,1)}, bf16[152,1280]{1,0:T(8,128)(2,1)}, bf16[2048,1280]{1,0:T(8,128)(2,1)}, bf16[4864,1280]{1,0:T(8,128)(2,1)}) custom-call(bf16[2048,1280]{1,0:T(8,128)(2,1)} %get-tuple-element.32.refs_0_, bf16[2048,1280]{1,0:T(8,128)(2,1)} %bitcast.14, bf16[4864,1280]{1,0:T(8,128)(2,1)} %bitcast.15, ...), custom_call_target="tpu_custom_call" | custom-call | tf_op jit(solution)/shard_map/backward_2/pallas_call | solution.py:693
  530.7 171.5 %backward_3.1 = (bf16[2,40,4864]{2,1,0:T(8,128)(2,1)}, bf16[152,1280]{1,0:T(8,128)(2,1)}, f32[8,128]{1,0:T(8,128)}) custom-call(bf16[2048,1280]{1,0:T(8,128)(2,1)} %get-tuple-element.29.refs_0_, bf16[2048,1280]{1,0:T(8,128)(2,1)} %get-tuple-element.39.refs_1_, bf16[4864,1280]{1,0:T(8,128)(2,1)} %bitcast.17, f32[2048,4864]{1,0:T(8,128)} %get-tuple-element.41.refs_3_, ...), custom_call_target="tpu_custom_call" | custom-call | tf_op jit(solution)/shard_map/backward_3/pallas_call | solution.py:693
  702.2 0.0 copy-start.1
  702.2 1.3 slice.17
  704.1 0.0 copy-start
  704.2 0.0 copy-start.4
  704.2 0.0 copy-start.9
  704.2 1.3 fusion.15
  705.5 0.0 copy-done.1
  705.5 0.1 fusion.16
  705.5 0.0 copy-done
  705.5 0.1 copy-done.4
  705.6 0.1 copy-done.9
  705.7 0.0 copy-start.7
  705.7 0.0 copy-start.8
  705.8 4.3 fusion.8
  710.1 0.0 copy-done.2
  710.1 0.0 copy-done.6
  710.1 0.3 copy-done.7
  710.4 0.9 copy-done.8
  711.3 3.6 fusion.2
  (6 shorter events, 0.0 us)
Async XLA Ops:
  702.2 3.3 copy-start.1
  704.1 1.4 copy-start
  704.2 1.5 copy-start.4
  704.2 1.6 copy-start.9
  705.7 4.4 copy-start.2
  705.7 4.4 copy-start.3
  705.7 4.4 copy-start.5
  705.7 4.4 copy-start.6
  705.7 4.7 copy-start.7
  705.7 5.6 copy-start.8
